TPU v7x, 512 devices: a whole 4x4x16 slice. The times are simulated.
512 devices in a mesh: seq: 64 (over x, z), tensor: 8 (over y, core).
Axes of the slice: x: 4, y: 4, z: 16, core: 2. Of those that a mesh axis runs over, the one named last changes fastest.
Arguments:
- hidden: bfloat16 [8, 16384, 8192], P(None, 'seq', 'tensor'), may hold values from -160 to 160
- norm_gain: bfloat16 [8192], P('tensor'), may hold values from 0.25 to 1.75
- value_weight: bfloat16 [8192], P('tensor'), may hold values from -0.0625 to 0.0625
- rewards: float32 [8, 16384], P(None, 'seq'), may hold values from -6 to 6
- done_flags: int32 [8, 16384], P(None, 'seq'), may hold values 0 or 1
- valid_mask: int32 [8, 16384], P('tensor', 'seq'), may hold values 0 or 1
- new_logprob: float32 [8, 16384], P('tensor', 'seq'), may hold values from -1 to 1
- old_logprob: float32 [8, 16384], P('tensor', 'seq'), may hold values from -1 to 1
- discount: float32 [8], replicated, may hold values from 0.9 to 1
- trace_decay: float32 [8], replicated, may hold values from 0.9 to 1
- bootstrap: float32 [8], replicated, may hold values from -5 to 5
Outputs:
- values: float32 [8, 16384], P('tensor', 'seq')
- white_adv: float32 [8, 16384], P('tensor', 'seq')
- token_loss: float32 [8, 16384], P('tensor', 'seq')
- policy_loss: float32 [], replicated
All inputs are finite; a program needn't handle non-finite values. No bound on the sum of `done_flags` or of `valid_mask` on one device may be relied on, other than what follows from the above.
Results may differ from a plain program's by a relative error of at most 0.00035.
Values sent between devices are 32-bit elements; how exact they have to be, the bound alone decides.
No kernel may reach another device: no remote copies, remote signals or barrier semaphores. Data moves between devices by JAX's collectives and lax.ppermute only.
A program may use at most 64 MiB of HBM per device.

v0:
```python
import jax
import jax.numpy as jnp
from jax import lax
from jax.sharding import Mesh
from jax.sharding import PartitionSpec as P

H = 8192
TENSOR = ("tensor_0", "tensor_1")
SEQ = ("seq_0", "seq_1")


EPS_NORM = 1e-06
EPS_WHITE = 1e-08
CLIP = 0.2
HIGHEST = lax.Precision.HIGHEST


def from_everyone(x, axis):
    devices = lax.axis_size(axis)
    return lax.all_to_all(jnp.broadcast_to(x[None], (devices, *x.shape)), axis, 0, 0, tiled=True)


def of_everyone(x, axis):
    everything = from_everyone(x, axis)
    return jnp.sum(everything, axis=0)


def packed_total(arrays, axis):
    vector, at, gathered = (jnp.concatenate([a.reshape(-1) for a in arrays]), 0, [])
    so_far = of_everyone(vector, axis)
    for a in arrays:
        gathered.append(so_far[at : at + a.size].reshape(a.shape))
        at += a.size
    return tuple(gathered)


def joined_along(tiles, dim):
    tiles = jnp.moveaxis(tiles, 0, dim)
    lengths = tiles.shape
    return tiles.reshape(*lengths[:dim], lengths[dim] * lengths[dim + 1], *lengths[dim + 2 :])


def gather_axes(x, axes, dim):
    far, near = axes
    tiles = from_everyone(from_everyone(x, far), near)
    return joined_along(tiles.swapaxes(0, 1).reshape(-1, *x.shape), dim)


def one_axis_at_a_time(x, axes):
    far, near = axes
    return of_everyone(of_everyone(x, near), far)


def compose(earlier, later):
    return (later[0] + later[1] * earlier[0], later[1] * earlier[1])


def local_pass(values, rewards, done_flags, discount, trace_decay):
    row_count, length = values.shape
    alive = 1.0 - done_flags.astype(jnp.float32)
    inner_next = jnp.concatenate([values[:, 1:], jnp.zeros((row_count, 1), jnp.float32)], axis=1)
    delta = rewards + discount[:, None] * alive * inner_next - values
    decay = discount * trace_decay
    counted = jnp.cumsum(done_flags, axis=1) - done_flags
    later_pos = lax.broadcasted_iota(jnp.int32, (length, length), 1)
    early_pos = lax.broadcasted_iota(jnp.int32, (length, length), 0)
    upper = later_pos >= early_pos
    distance = jnp.maximum(later_pos - early_pos, 0).astype(jnp.float32)
    powers = jnp.exp(distance[None, :, :] * jnp.log(decay)[:, None, None])
    same_episode = counted[:, None, :] == counted[:, :, None]
    weights = jnp.where(upper[None, :, :] & same_episode, powers, 0.0)
    local_adv = jnp.einsum(
        "stj,sj->st", weights, delta, precision=HIGHEST, preferred_element_type=jnp.float32
    )
    coef = weights[:, :, length - 1] * (discount * alive[:, length - 1])[:, None]
    return (local_adv, coef)


def fold_step(carry, block):
    return (compose(carry, block), carry)


def shards(
    hidden,
    norm_gain,
    value_weight,
    rewards,
    done_flags,
    valid_mask,
    new_logprob,
    old_logprob,
    discount,
    trace_decay,
    bootstrap,
):
    seqs_all = hidden.shape[0]
    own_rows = seqs_all // lax.axis_size(TENSOR)
    first_row = lax.axis_index(TENSOR) * own_rows
    scaled = norm_gain.astype(jnp.float32) * value_weight.astype(jnp.float32)
    squares = jnp.einsum("sth,sth->st", hidden, hidden, preferred_element_type=jnp.float32)
    products = jnp.einsum(
        "sth,h->st", hidden, scaled, precision=HIGHEST, preferred_element_type=jnp.float32
    )
    squares, products = packed_total((squares, products), TENSOR)
    values = products * lax.rsqrt(squares / H + EPS_NORM)
    local_adv, coef = local_pass(values, rewards, done_flags, discount, trace_decay)
    values_own = lax.dynamic_slice_in_dim(values, first_row, own_rows, 0)
    weight = valid_mask.astype(jnp.float32)
    offset = values[:, 0] + trace_decay * local_adv[:, 0]
    slope = trace_decay * coef[:, 0]
    local_own = lax.dynamic_slice_in_dim(local_adv, first_row, own_rows, 0)
    coef_own = lax.dynamic_slice_in_dim(coef, first_row, own_rows, 0)
    offset_own = lax.dynamic_slice_in_dim(offset, first_row, own_rows, 0)
    slope_own = lax.dynamic_slice_in_dim(slope, first_row, own_rows, 0)
    packed = jnp.stack(
        [
            offset_own,
            slope_own,
            jnp.sum(weight, axis=1),
            jnp.sum(weight * local_own, axis=1),
            jnp.sum(weight * coef_own, axis=1),
            jnp.sum(weight * local_own * local_own, axis=1),
            jnp.sum(weight * local_own * coef_own, axis=1),
            jnp.sum(weight * coef_own * coef_own, axis=1),
        ],
        axis=1,
    )
    gathered = gather_axes(packed[None], (("seq_0", "seq_1"), ("tensor_0", "tensor_1")), 0)
    seq_count = lax.axis_size(SEQ)
    table = gathered.reshape(seq_count, seqs_all, 8)
    start_pair = (jnp.zeros((seqs_all,), jnp.float32), jnp.ones((seqs_all,), jnp.float32))
    _, prefix = lax.scan(fold_step, start_pair, (table[:, :, 0], table[:, :, 1]), reverse=True)
    entering = prefix[0] + prefix[1] * bootstrap[None, :]
    count = jnp.sum(table[:, :, 2])
    total = jnp.sum(table[:, :, 3] + entering * table[:, :, 4])
    square_sum = jnp.sum(
        table[:, :, 5] + 2.0 * entering * table[:, :, 6] + entering * entering * table[:, :, 7]
    )
    mean = total / count
    variance = square_sum / count - mean * mean
    own_entering = lax.dynamic_slice_in_dim(
        lax.dynamic_index_in_dim(entering, lax.axis_index(SEQ), 0, False), first_row, own_rows, 0
    )
    adv_own = local_own + coef_own * own_entering[:, None]
    white_adv = (adv_own - mean) * lax.rsqrt(variance + EPS_WHITE)
    ratio = jnp.exp(new_logprob - old_logprob)
    surrogate = jnp.minimum(ratio * white_adv, jnp.clip(ratio, 1.0 - CLIP, 1.0 + CLIP) * white_adv)
    token_loss = -weight * surrogate
    loss_sum = one_axis_at_a_time(
        jnp.sum(token_loss), (("seq_0", "seq_1"), ("tensor_0", "tensor_1"))
    )
    policy_loss = loss_sum / count
    return (values_own, white_adv, token_loss, policy_loss)


def solution(mesh):
    split = Mesh(mesh.devices.reshape(4, 16, 4, 2), ("seq_0", "seq_1", "tensor_0", "tensor_1"))
    in_specs = (
        P(None, SEQ, TENSOR),
        P(TENSOR),
        P(TENSOR),
        P(None, SEQ),
        P(None, SEQ),
        P(TENSOR, SEQ),
        P(TENSOR, SEQ),
        P(TENSOR, SEQ),
        P(),
        P(),
        P(),
    )
    out_specs = (P(TENSOR, SEQ), P(TENSOR, SEQ), P(TENSOR, SEQ), P())
    return jax.shard_map(
        shards, mesh=split, in_specs=in_specs, out_specs=out_specs, check_vma=False
    )
```

profile of v0, /device:TPU:1, one launch (start us, length us, event | category | flops | bytes accessed | tf_op | source)
XLA Modules:
  0.0 119.2 jit_solution(13456207747296009241)
XLA Ops:
  0.7 3.2 %fusion.3 = f32[8,256]{1,0:T(8,128)S(1)} fusion(bf16[8,256,1024]{2,1,0:T(8,128)(2,1)} %param.13), kind=kLoop, calls=%fused_computation.9 | loop fusion | flops 6289408 | bytes 4202496 | tf_op jit(solution)/shard_map/sth,sth->st/dot_general | solution.py:100
  4.1 3.3 %fusion.15 = f32[1,8,256]{2,0,1:T(1,128)S(1)} fusion(f32[1024,1,1]{0,1,2:T(1,128)S(1)} %bitcast.78, bf16[8,256,1024]{2,1,0:T(8,128)(2,1)S(1)} %copy-done), kind=kOutput, calls=%fused_computation.57 | convolution fusion | flops 25165824 | bytes 4206592 | tf_op jit(solution)/shard_map/sth,h->st/dot_general | solution.py:101
  7.5 0.7 broadcast_in_dim.65
  8.2 10.1 %all-to-all-start = ((f32[8,1,4096]{2,1,0:T(1,128)}), f32[8,1,4096]{2,1,0:T(1,128)S(1)}, u32[]{:S(2)}, u32[]{:S(2)}) async-start(f32[8,1,4096]{2,1,0:T(1,128)} %broadcast_in_dim.65), calls=%async_computation | async-start | bytes 262144 | tf_op jit(solution)/shard_map/all_to_all | solution.py:20
  18.3 0.6 reduce-window.6
  18.9 0.2 slice_reduce_fusion
  19.5 4.1 %all-to-all-done = f32[8,1,4096]{2,1,0:T(1,128)S(1)} async-done(((f32[8,1,4096]{2,1,0:T(1,128)}), f32[8,1,4096]{2,1,0:T(1,128)S(1)}, u32[]{:S(2)}, u32[]{:S(2)}) %all-to-all-start) | async-done | bytes 131104 | tf_op jit(solution)/shard_map/all_to_all | solution.py:20
  24.2 0.7 exponential_select_fusion
  25.0 1.7 %fusion.4 = f32[8,1,256]{2,1,0:T(1,128)S(1)} fusion(f32[8,256,256]{1,0,2:T(8,128)S(1)} %exponential_select_fusion, f32[8,256,1]{1,0,2:T(8,128)S(1)} %get-tuple-element.232), kind=kOutput, calls=%fused_computation.10 | convolution fusion | flops 6291456 | bytes 2113536 | tf_op jit(solution)/shard_map/stj,sj->st/dot_general | solution.py:72
  26.9 0.6 dynamic_slice.43
  27.5 0.6 dynamic_slice.42
  28.1 0.7 multiply_reduce_fusion
  28.8 5.2 %stack.35 = f32[1,8]{1,0:T(1,128)S(1)} concatenate(f32[1,1]{1,0:T(1,128)} %bitcast.7, f32[1,1]{1,0:T(1,128)} %bitcast.8, f32[1,1]{1,0:T(1,128)} %bitcast.9, f32[1,1]{1,0:T(1,128)} %bitcast.10, f32[1,1]{1,0:T(1,128)} %bitcast.11, f32[1,1]{1,0:T(1,128)} %bitcast.12, f32[1,1]{1,0:T(1,128)} %bitcast.13, f32[1,1]{1,0:T(1,128)} %bitcast.14), dimensions={1} | concatenate | bytes 64 | tf_op jit(solution)/shard_map/stack | solution.py:115
  34.0 27.2 %all_to_all.28 = f32[64,1,1,8]{3,2,1,0:T(1,128)S(1)} all-to-all(f32[64,1,1,8]{3,2,1,0:T(1,128)S(1)} %broadcast_in_dim.68), channel_id=1, replica_groups=mesh['seq_0'=4,'seq_1'=16,'tensor_0'=4,'tensor_1'=2] {'seq_0','seq_1'}, dimensions={0} | all-to-all | bytes 4096 | tf_op jit(solution)/shard_map/all_to_all | solution.py:20
  61.3 0.7 reshape.119
  62.0 5.5 %all-to-all-start.2 = ((f32[8,1,512]{2,1,0:T(1,128)}), f32[8,1,512]{2,1,0:T(1,128)S(1)}, u32[]{:S(2)}, u32[]{:S(2)}) async-start(f32[8,1,512]{2,1,0:T(1,128)} %reshape.119), calls=%async_computation.2 | async-start | bytes 32768 | tf_op jit(solution)/shard_map/all_to_all | solution.py:20
  67.5 4.7 %all-to-all-done.2 = f32[8,1,512]{2,1,0:T(1,128)S(1)} async-done(((f32[8,1,512]{2,1,0:T(1,128)}), f32[8,1,512]{2,1,0:T(1,128)S(1)}, u32[]{:S(2)}, u32[]{:S(2)}) %all-to-all-start.2) | async-done | bytes 16416 | tf_op jit(solution)/shard_map/all_to_all | solution.py:20
  72.2 0.5 broadcast.79
  72.7 0.7 reduce.22
  73.5 0.6 slice_reduce_fusion.1
  74.3 7.4 %while.21 = (s32[]{:T(128)}, f32[8]{0:T(128)S(1)}, f32[8]{0:T(128)S(1)}, f32[64,8]{1,0:T(8,128)S(1)}, f32[64,8]{1,0:T(8,128)S(1)}, /*index=5*/f32[64,8]{1,0:T(8,...) while((s32[]{:T(128)}, f32[8]{0:T(128)S(1)}, f32[8]{0:T(128)S(1)}, ...), condition=%wide.region_10.11_spmd.clone, body=%wide.region_9.10_spmd.clone.sunk | while | flops 44 | bytes 519 | solution.py:132
  81.8 0.7 add_reduce_fusion.1
  85.2 0.6 dynamic_slice.44
  85.8 1.9 %fusion.12 = (f32[]{:T(128)}, f32[1,256]{1,0:T(1,128)}, f32[1,256]{1,0:T(1,128)}) fusion(f32[1,256]{1,0:T(1,128)S(1)} %copy-done.8, f32[1,256]{1,0:T(1,128)S(1)} %copy-done.9, s32[1,256]{1,0:T(1,128)S(1)} %copy-done.3, f32[]{:T(128)S(6)} %rsqrt.8, f32[]{:T(128)S(6)} %div.17, f32[]{:T(128)} %bitcast.22, f32[8,256]{1,0:T(8,128)S(1)} %fusion.6, ...), kind=kLoop, calls=%fused_computation.52 | loop fusion | flops 3327 | bytes 7188 | tf_op jit(solution)/shard_map/reduce_sum | solution.py:150
  87.7 0.7 broadcast_in_dim.71
  88.4 7.7 %all_to_all.29 = f32[8,1,1]{2,1,0:T(1,128)S(1)} all-to-all(f32[8,1,1]{2,1,0:T(1,128)S(1)} %broadcast_in_dim.71), channel_id=1, replica_groups=mesh['seq_0'=4,'seq_1'=16,'tensor_0'=4,'tensor_1'=2] {'tensor_0','tensor..., dimensions={0} | all-to-all | bytes 64 | tf_op jit(solution)/shard_map/all_to_all | solution.py:20
  96.1 0.6 reduce_sum.128
  96.7 1.3 %broadcast_in_dim.72 = f32[64,1,1]{2,1,0:T(1,128)} broadcast(f32[]{:T(128)} %reduce_sum.128), dimensions={} | broadcast | bytes 260 | tf_op jit(solution)/shard_map/broadcast_in_dim | solution.py:20
  98.0 4.6 %all-to-all-start.4 = ((f32[64,1,1]{2,1,0:T(1,128)}), f32[64,1,1]{2,1,0:T(1,128)S(1)}, u32[]{:S(2)}, u32[]{:S(2)}) async-start(f32[64,1,1]{2,1,0:T(1,128)} %broadcast_in_dim.72), calls=%async_computation.4 | async-start | bytes 65536 | tf_op jit(solution)/shard_map/all_to_all | solution.py:20
  102.6 0.6 constant_dynamic-slice_fusion.3
  103.1 12.8 %all-to-all-done.4 = f32[64,1,1]{2,1,0:T(1,128)S(1)} async-done(((f32[64,1,1]{2,1,0:T(1,128)}), f32[64,1,1]{2,1,0:T(1,128)S(1)}, u32[]{:S(2)}, u32[]{:S(2)}) %all-to-all-start.4) | async-done | bytes 288 | tf_op jit(solution)/shard_map/all_to_all | solution.py:20
  115.9 0.7 reduce_sum.129
  (250 shorter events, 7.8 us)
Async XLA Ops:
  0.6 3.5 %copy-start = (bf16[8,256,1024]{2,1,0:T(8,128)(2,1)S(1)}, bf16[8,256,1024]{2,1,0:T(8,128)(2,1)}, u32[]{:S(2)}) copy-start(bf16[8,256,1024]{2,1,0:T(8,128)(2,1)} %param.13) | copy-start | bytes 12582916
  0.6 3.2 %copy-start.7 = (bf16[1024]{0:T(1024)(128)(2,1)S(1)}, bf16[1024]{0:T(1024)(128)(2,1)}, u32[]{:S(2)}) copy-start(bf16[1024]{0:T(1024)(128)(2,1)} %param.14) | copy-start | bytes 6148
  0.7 3.2 %copy-start.6 = (bf16[1024]{0:T(1024)(128)(2,1)S(1)}, bf16[1024]{0:T(1024)(128)(2,1)}, u32[]{:S(2)}) copy-start(bf16[1024]{0:T(1024)(128)(2,1)} %param.15) | copy-start | bytes 6148
  4.1 14.2 %copy-start.1 = (s32[8,256]{1,0:T(8,128)S(1)}, s32[8,256]{1,0:T(8,128)}, u32[]{:S(2)}) copy-start(s32[8,256]{1,0:T(8,128)} %param.17) | copy-start | bytes 24580
  4.1 19.8 %copy-start.2 = (f32[8,256]{1,0:T(8,128)S(1)}, f32[8,256]{1,0:T(8,128)}, u32[]{:S(2)}) copy-start(f32[8,256]{1,0:T(8,128)} %param.16) | copy-start | bytes 24580
  4.1 19.8 %copy-start.4 = (f32[8]{0:T(128)S(1)}, f32[8]{0:T(128)}, u32[]{:S(2)}) copy-start(f32[8]{0:T(128)} %param.21) | copy-start | bytes 100
  4.1 20.1 %copy-start.5 = (f32[8]{0:T(128)S(1)}, f32[8]{0:T(128)}, u32[]{:S(2)}) copy-start(f32[8]{0:T(128)} %param.22) | copy-start | bytes 100
  8.2 15.4 %all-to-all-start = ((f32[8,1,4096]{2,1,0:T(1,128)}), f32[8,1,4096]{2,1,0:T(1,128)S(1)}, u32[]{:S(2)}, u32[]{:S(2)}) async-start(f32[8,1,4096]{2,1,0:T(1,128)} %broadcast_in_dim.65), calls=%async_computation | async-start | bytes 262144 | tf_op jit(solution)/shard_map/all_to_all | solution.py:20
  24.2 3.9 %copy-start.3 = (s32[1,256]{1,0:T(1,128)S(1)}, s32[1,256]{1,0:T(1,128)}, u32[]{:S(2)}) copy-start(s32[1,256]{1,0:T(1,128)} %param.18) | copy-start | bytes 3076
  24.9 56.9 %copy-start.10 = (f32[8]{0:T(128)S(1)}, f32[8]{0:T(128)}, u32[]{:S(2)}) copy-start(f32[8]{0:T(128)} %param.23) | copy-start | bytes 100
  24.9 60.9 %copy-start.8 = (f32[1,256]{1,0:T(1,128)S(1)}, f32[1,256]{1,0:T(1,128)}, u32[]{:S(2)}) copy-start(f32[1,256]{1,0:T(1,128)} %param.19) | copy-start | bytes 3076
  25.0 60.9 %copy-start.9 = (f32[1,256]{1,0:T(1,128)S(1)}, f32[1,256]{1,0:T(1,128)}, u32[]{:S(2)}) copy-start(f32[1,256]{1,0:T(1,128)} %param.20) | copy-start | bytes 3076
  62.0 10.2 %all-to-all-start.2 = ((f32[8,1,512]{2,1,0:T(1,128)}), f32[8,1,512]{2,1,0:T(1,128)S(1)}, u32[]{:S(2)}, u32[]{:S(2)}) async-start(f32[8,1,512]{2,1,0:T(1,128)} %reshape.119), calls=%async_computation.2 | async-start | bytes 32768 | tf_op jit(solution)/shard_map/all_to_all | solution.py:20
  98.0 18.0 %all-to-all-start.4 = ((f32[64,1,1]{2,1,0:T(1,128)}), f32[64,1,1]{2,1,0:T(1,128)S(1)}, u32[]{:S(2)}, u32[]{:S(2)}) async-start(f32[64,1,1]{2,1,0:T(1,128)} %broadcast_in_dim.72), calls=%async_computation.4 | async-start | bytes 65536 | tf_op jit(solution)/shard_map/all_to_all | solution.py:20
where the time goes:
time: 120 us; the launch traced here: 119 us
  blocking collectives  34.9 us (29%)
  waiting for transfers between devices  21.6 us (18%)
  starting transfers between devices  20.2 us (17%)
  local copies, waits for them, and re-layouts  17.8 us (15%)
  other arithmetic  12.1 us (10%)
  between operations  6.11 us (5%)
  matrix products  5.08 us (4%)
  loops' own time  1.38 us (1%)
    all_to_all x2, blocking collectives, from_everyone(): lax.all_to_all(jnp.broadcast_to(x[None], (devices, *x.shape)), axis, 0, 0...  34.9 us
    all_to_all x3, waiting for transfers between devices, from_everyone(): lax.all_to_all(jnp.broadcast_to(x[None], (devices, *x.shape)), axis, 0, 0...  21.6 us
    all_to_all x3, starting transfers between devices, from_everyone(): lax.all_to_all(jnp.broadcast_to(x[None], (devices, *x.shape)), axis, 0, 0...  20.2 us
    another operation x1, local copies, waits for them, and re-layouts, shards(): jnp.stack([offset_own, slope_own, jnp.sum(weight, axis=1), jnp.sum(weight...  5.2 us
    dynamic_update_slice x128, local copies, waits for them, and re-layouts, shards(): lax.scan(fold_step, start_pair, (table[:, :, 0], table[:, :, 1]), reverse...  4.78 us
    dot_general x1, matrix products, shards(): jnp.einsum('sth,h->st', hidden, scaled, precision=HIGHEST, preferred_elem...  3.34 us
    dot_general x1, other arithmetic, shards(): jnp.einsum('sth,sth->st', hidden, hidden, preferred_element_type=jnp.floa...  3.22 us
    broadcast_in_dim x5, local copies, waits for them, and re-layouts, from_everyone(): jnp.broadcast_to(x[None], (devices, *x.shape))  2.74 us
  transfers between devices with their start and end apart: 3, of which 3 were waited for; matrix products, arithmetic and copies ran while one was open for 1% of the time, Pallas kernels for 0%

commit v1 on v0

v1 whole, which is shorter than its diff:
```python
import jax
import jax.numpy as jnp
from jax import lax
from jax.experimental import pallas as pl
from jax.experimental.pallas import tpu as pltpu
from jax.sharding import PartitionSpec as P

EPS_NORM = 1e-06
EPS_WHITE = 1e-08
CLIP = 0.2

HEAD_ROWS = 40
TOKEN_ROWS = 5
WIDTH = 16
OFFSET, SLOPE, COUNT, MEAN_L, MEAN_C, VAR_L, COV, VAR_C, LAST_DONE = range(9)

CONTRACT_LANES = (((1,), (1,)), ((), ()))


def head_kernel(gain_ref, weight_ref, mask_ref, hidden_ref, out_ref, held, arrived):
    rollouts, length, width = held.shape
    peers = out_ref.shape[0] // HEAD_ROWS
    copies = [
        pltpu.make_async_copy(hidden_ref.at[r], held.at[r], arrived.at[r]) for r in range(rollouts)
    ]
    for copy in copies:
        copy.start()
    scaled = gain_ref[...].astype(jnp.float32) * weight_ref[...].astype(jnp.float32)
    coarse = scaled.astype(jnp.bfloat16).astype(jnp.float32)
    fine = scaled - coarse
    row = lax.broadcasted_iota(jnp.int32, (8, 128), 0)
    tiles = []
    for j in range(width // 128):
        tile = jnp.where(row == 0, coarse[j : j + 1, :], 0.0)
        tiles.append(jnp.where(row == 1, fine[j : j + 1, :], tile))
    lhs = jnp.concatenate(tiles, axis=1).astype(jnp.bfloat16)
    ones = jnp.ones((8, 256), jnp.bfloat16)
    mask = mask_ref[...].astype(jnp.float32)
    out_ref[32:33, :] = mask[:, :128]
    out_ref[33:34, :] = mask[:, 128:]
    out_ref[34:40, :] = jnp.zeros((6, 128), jnp.float32)
    for r in range(rollouts):
        copies[r].wait()
        block = held[r]
        products = lax.dot_general(lhs, block, CONTRACT_LANES, preferred_element_type=jnp.float32)
        products = products[0:1, :] + products[1:2, :]
        total = jnp.zeros((length, 128), jnp.float32)
        for j in range(width // 128):
            wide = held[r, :, 128 * j : 128 * (j + 1)].astype(jnp.float32)
            total = total + wide * wide
        high = total.astype(jnp.bfloat16)
        low = (total - high.astype(jnp.float32)).astype(jnp.bfloat16)
        squares = lax.dot_general(
            ones,
            jnp.concatenate([high, low], axis=1),
            CONTRACT_LANES,
            preferred_element_type=jnp.float32,
        )
        out_ref[r : r + 1, :] = squares[0:1, :128]
        out_ref[8 + r : 9 + r, :] = squares[0:1, 128:]
        out_ref[16 + r : 17 + r, :] = products[:, :128]
        out_ref[24 + r : 25 + r, :] = products[:, 128:]
    own = out_ref[0:HEAD_ROWS, :]
    for peer in range(1, peers):
        out_ref[HEAD_ROWS * peer : HEAD_ROWS * (peer + 1), :] = own


def column(ref, shape):
    row = lax.broadcasted_iota(jnp.int32, shape, 0)
    out = jnp.full(shape, ref[0], jnp.float32)
    for r in range(1, shape[0]):
        out = jnp.where(row == r, ref[r], out)
    return out


def lane_sum(x):
    return jnp.sum(x, axis=1, keepdims=True)


def local_kernel(
    hidden_width,
    discount_ref,
    trace_ref,
    recv_ref,
    rewards_ref,
    done_ref,
    new_ref,
    old_ref,
    mask_ref,
    values_ref,
    out_ref,
):
    me = lax.axis_index("tensor")
    rollouts, length = rewards_ref.shape
    peers = recv_ref.shape[0] // HEAD_ROWS
    shape = (rollouts, length)
    total = recv_ref[0:32, :]
    for peer in range(1, peers):
        total = total + recv_ref[HEAD_ROWS * peer : HEAD_ROWS * peer + 32, :]
    squares = jnp.concatenate([total[0:8], total[8:16]], axis=1)
    products = jnp.concatenate([total[16:24], total[24:32]], axis=1)
    weight = jnp.concatenate(
        [
            recv_ref[pl.ds(32, peers, stride=HEAD_ROWS), :],
            recv_ref[pl.ds(33, peers, stride=HEAD_ROWS), :],
        ],
        axis=1,
    )
    values = products * lax.rsqrt(squares / hidden_width + EPS_NORM)
    discount, trace = column(discount_ref, shape), column(trace_ref, shape)
    alive = 1.0 - done_ref[...].astype(jnp.float32)
    lane = lax.broadcasted_iota(jnp.int32, shape, 1)
    inner_next = jnp.where(lane < length - 1, pltpu.roll(values, length - 1, 1), 0.0)
    local = rewards_ref[...] + discount * alive * inner_next - values
    chain = discount * trace * alive
    step = 1
    while step < length:
        inside = lane < length - step
        local_later = jnp.where(inside, pltpu.roll(local, length - step, 1), 0.0)
        chain_later = jnp.where(inside, pltpu.roll(chain, length - step, 1), 1.0)
        local = local + chain * local_later
        chain = chain * chain_later
        step *= 2
    coef = chain / trace
    count = lane_sum(weight)
    safe = 1.0 / jnp.maximum(count, 1.0)
    mean_l = lane_sum(weight * local) * safe
    mean_c = lane_sum(weight * coef) * safe
    off_l = weight * (local - mean_l)
    off_c = weight * (coef - mean_c)
    stats = {
        OFFSET: values[:, 0:1] + trace[:, 0:1] * local[:, 0:1],
        SLOPE: chain[:, 0:1],
        COUNT: count,
        MEAN_L: mean_l,
        MEAN_C: mean_c,
        VAR_L: lane_sum(off_l * off_l),
        COV: lane_sum(off_l * off_c),
        VAR_C: lane_sum(off_c * off_c),
        LAST_DONE: jnp.max(
            jnp.where(alive > 0.5, -1.0, lane.astype(jnp.float32)), axis=1, keepdims=True
        ),
    }
    small_lane = lax.broadcasted_iota(jnp.int32, (rollouts, 128), 1)
    summary = jnp.zeros((rollouts, 128), jnp.float32)
    for at, stat in stats.items():
        summary = jnp.where(small_lane == at, stat, summary)
    summary = pltpu.roll(summary, 0, 1, stride=WIDTH, stride_axis=0)
    summary = jnp.sum(summary, axis=0, keepdims=True)
    mine = lax.broadcasted_iota(jnp.int32, shape, 0) == me
    own_local = jnp.sum(jnp.where(mine, local, 0.0), axis=0, keepdims=True)
    values_ref[...] = jnp.sum(jnp.where(mine, values, 0.0), axis=0, keepdims=True)
    ratio = mask_ref[...].astype(jnp.float32) * jnp.exp(new_ref[...] - old_ref[...])
    row = lax.broadcasted_iota(jnp.int32, (8, 128), 0)
    message = jnp.where(row == 0, summary, 0.0)
    message = jnp.where(row == 1, own_local[:, :128], message)
    message = jnp.where(row == 2, own_local[:, 128:], message)
    message = jnp.where(row == 3, ratio[:, :128], message)
    message = jnp.where(row == 4, ratio[:, 128:], message)
    for peer in range(out_ref.shape[0] // TOKEN_ROWS):
        out_ref[TOKEN_ROWS * peer : TOKEN_ROWS * (peer + 1), :] = message[0:TOKEN_ROWS, :]


def full_sum(x):
    return jnp.sum(jnp.sum(x, axis=0, keepdims=True), axis=1, keepdims=True)


def final_kernel(
    discount_ref, trace_ref, bootstrap_ref, recv_ref, white_ref, loss_ref, out_ref
):
    tensor, seq = lax.axis_index("tensor"), lax.axis_index("seq")
    blocks = recv_ref.shape[0] // TOKEN_ROWS
    rollouts = out_ref.shape[0]
    shape = (blocks, 128)
    table = recv_ref[pl.ds(0, blocks, stride=TOKEN_ROWS), :]
    row = lax.broadcasted_iota(jnp.int32, shape, 0)
    lane = lax.broadcasted_iota(jnp.int32, shape, 1)

    def stat(at):
        return pltpu.roll(table, 128 - at, 1)

    start = jnp.full(shape, bootstrap_ref[0], jnp.float32)
    for r in range(1, rollouts):
        start = jnp.where(lane == WIDTH * r, bootstrap_ref[r], start)
    last = row == blocks - 1
    offset = jnp.where(last, start, pltpu.roll(table, blocks - 1, 0))
    slope = jnp.where(last, 0.0, pltpu.roll(stat(SLOPE), blocks - 1, 0))
    step = 1
    while step < blocks:
        inside = row < blocks - step
        offset_later = jnp.where(inside, pltpu.roll(offset, blocks - step, 0), 0.0)
        slope_later = jnp.where(inside, pltpu.roll(slope, blocks - step, 0), 0.0)
        offset = offset + slope * offset_later
        slope = slope * slope_later
        step *= 2
    entering = offset
    used = (lane % WIDTH == 0) & (lane < WIDTH * rollouts)
    members = jnp.where(used, stat(COUNT), 0.0)
    block_mean = jnp.where(used, stat(MEAN_L) + entering * stat(MEAN_C), 0.0)
    count = full_sum(members)
    mean = full_sum(members * block_mean) / count
    within = stat(VAR_L) + entering * (2.0 * stat(COV) + entering * stat(VAR_C))
    apart = block_mean - mean
    variance = full_sum(jnp.where(used, within, 0.0) + members * apart * apart) / count
    scale = lax.rsqrt(variance + EPS_WHITE)

    mine = lane == WIDTH * tensor
    own_entering = lane_sum(jnp.where(mine, entering, 0.0))
    own_done = lane_sum(jnp.where(mine, stat(LAST_DONE), 0.0))
    discount = discount_ref[tensor]
    decay = discount * trace_ref[tensor]
    loss = jnp.zeros(shape, jnp.float32)
    own = pl.ds(TOKEN_ROWS * seq, 1)
    for half in range(2):
        position = lax.broadcasted_iota(jnp.int32, (1, 128), 1) + 128 * half
        left = 255 - position
        power, factor = jnp.full((1, 128), discount, jnp.float32), jnp.full((1, 128), decay)
        for bit in range(8):
            power = jnp.where((left >> bit) & 1 == 1, power * factor, power)
            factor = factor * factor
        coef = jnp.where(position.astype(jnp.float32) > own_done, power, 0.0)
        local = recv_ref[pl.ds(1 + half, blocks, stride=TOKEN_ROWS), :]
        ratio = recv_ref[pl.ds(3 + half, blocks, stride=TOKEN_ROWS), :]
        white = (local + coef * own_entering - mean) * scale
        clipped = jnp.clip(ratio, 1.0 - CLIP, 1.0 + CLIP)
        token = jnp.where(ratio > 0.0, -jnp.minimum(ratio * white, clipped * white), 0.0)
        loss = loss + token
        mine_row = row == seq
        white_ref[:, 128 * half : 128 * (half + 1)] = jnp.sum(
            jnp.where(mine_row, white, 0.0), axis=0, keepdims=True
        )
        loss_ref[:, 128 * half : 128 * (half + 1)] = jnp.sum(
            jnp.where(mine_row, token, 0.0), axis=0, keepdims=True
        )
    out_ref[...] = jnp.broadcast_to(full_sum(loss) / count, out_ref.shape)


VMEM = pl.BlockSpec(memory_space=pltpu.VMEM)
SMEM = pl.BlockSpec(memory_space=pltpu.SMEM)
ANY = pl.BlockSpec(memory_space=pl.ANY)


def exchange(x, axis):
    return lax.all_to_all(x, axis, 0, 0, tiled=True)


def shards(
    hidden,
    norm_gain,
    value_weight,
    rewards,
    done_flags,
    valid_mask,
    new_logprob,
    old_logprob,
    discount,
    trace_decay,
    bootstrap,
):
    rollouts, length, width = hidden.shape
    peers, blocks = lax.axis_size("tensor"), lax.axis_size("seq")
    f32 = jnp.float32
    sent = pl.pallas_call(
        head_kernel,
        out_shape=jax.ShapeDtypeStruct((peers * HEAD_ROWS, 128), f32),
        in_specs=[VMEM, VMEM, VMEM, ANY],
        out_specs=VMEM,
        scratch_shapes=[
            pltpu.VMEM(hidden.shape, hidden.dtype),
            pltpu.SemaphoreType.DMA((rollouts,)),
        ],
        name="head",
    )(
        norm_gain.reshape(-1, 128),
        value_weight.reshape(-1, 128),
        valid_mask,
        hidden,
    )
    got = exchange(sent.reshape(peers, 1, HEAD_ROWS * 128), "tensor")
    own_row = jax.ShapeDtypeStruct((1, length), f32)
    values, sent = pl.pallas_call(
        lambda *refs: local_kernel(width * peers, *refs),
        out_shape=(own_row, jax.ShapeDtypeStruct((blocks * TOKEN_ROWS, 128), f32)),
        in_specs=[SMEM, SMEM] + [VMEM] * 6,
        out_specs=(VMEM, VMEM),
        name="local",
    )(
        discount,
        trace_decay,
        got.reshape(peers * HEAD_ROWS, 128),
        rewards,
        done_flags,
        new_logprob,
        old_logprob,
        valid_mask,
    )
    got = exchange(sent.reshape(blocks, 1, TOKEN_ROWS * 128), "seq")
    white, loss, sent = pl.pallas_call(
        final_kernel,
        out_shape=(own_row, own_row, jax.ShapeDtypeStruct((peers, 128), f32)),
        in_specs=[SMEM, SMEM, SMEM, VMEM],
        out_specs=(VMEM, VMEM, VMEM),
        name="final",
    )(discount, trace_decay, bootstrap, got.reshape(blocks * TOKEN_ROWS, 128))
    got = exchange(sent.reshape(peers, 1, 128), "tensor")
    return values, white, loss, jnp.sum(got[:, 0, 0])


def solution(mesh):
    in_specs = (
        P(None, "seq", "tensor"),
        P("tensor"),
        P("tensor"),
        P(None, "seq"),
        P(None, "seq"),
        P("tensor", "seq"),
        P("tensor", "seq"),
        P("tensor", "seq"),
        P(),
        P(),
        P(),
    )
    out_specs = (P("tensor", "seq"), P("tensor", "seq"), P("tensor", "seq"), P())
    return jax.shard_map(
        shards, mesh=mesh, in_specs=in_specs, out_specs=out_specs, check_vma=False
    )
```

time: 120 us -> 67.4 us (0.56)
  waiting for transfers between devices: 21.6 us -> 0 us
  blocking collectives: 34.9 us -> 55.8 us
  starting transfers between devices: 20.2 us -> 0 us
  local copies, waits for them, and re-layouts: 17.8 us -> 0 us
  other arithmetic: 12.1 us -> 0.61 us
  Pallas kernels: 0 us -> 9.99 us
  between operations: 6.11 us -> 0.64 us
  matrix products: 5.08 us -> 0 us
  loops' own time: 1.38 us -> 0 us
    all_to_all x3 -> x0, waiting for transfers between devices: 21.6 us -> none  [from_everyone(): lax.all_to_all(jnp.broadcast_to(x[None], (devices, *x.shape)), axis, 0, 0...]
    all_to_all x2 -> x3, blocking collectives: 34.9 us -> 55.8 us  [exchange(): return lax.all_to_all(x, axis, 0, 0, tiled=True)]
    all_to_all x3 -> x0, starting transfers between devices: 20.2 us -> none  [from_everyone(): lax.all_to_all(jnp.broadcast_to(x[None], (devices, *x.shape)), axis, 0, 0...]
    pallas_call x0 -> x3, Pallas kernels: none -> 9.99 us  [the longest x1 5.6 us: shards(): pl.pallas_call(head_kernel, out_shape=jax.ShapeDtypeStruct((peers * HEAD_...]
    another operation x5 -> x0, local copies, waits for them, and re-layouts: 5.21 us -> none  [the longest x1 5.2 us: shards(): jnp.stack([offset_own, slope_own, jnp.sum(weight, axis=1), jnp.sum(weight...]
    dot_general x2 -> x0, matrix products: 5.08 us -> none  [the longest x1 3.34 us: shards(): jnp.einsum('sth,h->st', hidden, scaled, precision=HIGHEST, preferred_elem...]
    dynamic_update_slice x128 -> x0, local copies, waits for them, and re-layouts: 4.78 us -> none  [shards(): lax.scan(fold_step, start_pair, (table[:, :, 0], table[:, :, 1]), reverse...]
    reduce_sum x7 -> x1, other arithmetic: 5.38 us -> 0.61 us  [shards(): return (values, white, loss, jnp.sum(got[:, 0, 0]))]
  transfers between devices with their start and end apart: 3 -> 0, of which waited for: 3 -> 0; matrix products, arithmetic and copies ran while one was open for 1% -> 0% of each run, Pallas kernels for 0% -> 0%
where the time goes in v1:
time: 67.4 us; the launch traced here: 67 us
  blocking collectives  55.8 us (83%)
  Pallas kernels  9.99 us (15%)
    all_to_all x3, blocking collectives, exchange(): return lax.all_to_all(x, axis, 0, 0, tiled=True)  55.8 us
    pallas_call x1, Pallas kernels, shards(): pl.pallas_call(head_kernel, out_shape=jax.ShapeDtypeStruct((peers * HEAD_...  5.6 us
    pallas_call x1, Pallas kernels, shards(): pl.pallas_call(lambda *refs: local_kernel(width * peers, *refs), out_shap...  2.47 us
    pallas_call x1, Pallas kernels, shards(): pl.pallas_call(final_kernel, out_shape=(own_row, own_row, jax.ShapeDtypeS...  1.92 us

profile of v1, /device:TPU:1, one launch (start us, length us, event | category | flops | bytes accessed | tf_op | source)
XLA Modules:
  0.0 67.0 jit_solution(17925068222677906246)
XLA Ops:
  0.6 5.6 %head.1 = f32[320,128]{1,0:T(8,128)} custom-call(bf16[8,128]{1,0:T(8,128)(2,1)} %bitcast.14, bf16[8,128]{1,0:T(8,128)(2,1)} %bitcast.15, s32[1,256]{1,0:T(1,128)} %refs_7_.1, bf16[8,256,1024]{2,1,0:T(8,128)(2,1)} %hidden_ref.1), custom_call_target="tpu_custom_call" | custom-call | tf_op jit(solution)/shard_map/head/pallas_call | solution.py:263
  6.2 16.4 %all_to_all.15 = f32[8,1,5120]{2,1,0:T(1,128)} all-to-all(f32[8,1,5120]{2,1,0:T(1,128)} %bitcast.9), channel_id=1, replica_groups=mesh['seq'=64,'tensor'=8] {'tensor'}, dimensions={0} | all-to-all | bytes 327680 | tf_op jit(solution)/shard_map/all_to_all | solution.py:244
  22.6 2.5 %local.1 = (f32[1,256]{1,0:T(1,128)}, f32[320,128]{1,0:T(8,128)}) custom-call(f32[8]{0:T(128)} %discount_ref.1, f32[8]{0:T(128)} %trace_ref.1, f32[320,128]{1,0:T(8,128)} %bitcast.11, f32[8,256]{1,0:T(8,128)} %refs_3_.1, s32[8,256]{1,0:T(8,128)} %refs_4_.1, f32[1,256]{1,0:T(1,128)} %refs_5_.1, f32[1,256]{1,0:T(1,128)} %refs_6_.1, s32[1,256]{1,0:T(1,128)} %refs_7_.1), custom_call_target="tpu_custom_call" | custom-call | tf_op jit(solution)/shard_map/local/pallas_call | solution.py:281
  25.1 28.7 %all_to_all.16 = f32[64,1,640]{2,1,0:T(1,128)} all-to-all(f32[64,1,640]{2,1,0:T(1,128)} %bitcast.12), channel_id=1, replica_groups=mesh['seq'=64,'tensor'=8] {'seq'}, dimensions={0} | all-to-all | bytes 327680 | tf_op jit(solution)/shard_map/all_to_all | solution.py:244
  53.8 1.9 %final.1 = (f32[1,256]{1,0:T(1,128)}, f32[1,256]{1,0:T(1,128)}, f32[8,128]{1,0:T(8,128)}) custom-call(f32[8]{0:T(128)} %discount_ref.1, f32[8]{0:T(128)} %trace_ref.1, f32[8]{0:T(128)} %bootstrap_ref.1, f32[320,128]{1,0:T(8,128)} %bitcast.10), custom_call_target="tpu_custom_call" | custom-call | tf_op jit(solution)/shard_map/final/pallas_call | solution.py:298
  55.7 10.7 %all_to_all.17 = f32[8,1,128]{2,1,0:T(1,128)S(1)} all-to-all(f32[8,1,128]{2,1,0:T(1,128)} %bitcast.13), channel_id=1, replica_groups=mesh['seq'=64,'tensor'=8] {'tensor'}, dimensions={0} | all-to-all | bytes 8192 | tf_op jit(solution)/shard_map/all_to_all | solution.py:244
  66.4 0.6 slice_reduce_fusion

commit v2 on v1

v2 whole, which is shorter than its diff:
```python
import jax
import jax.numpy as jnp
from jax import lax
from jax.experimental import pallas as pl
from jax.experimental.pallas import tpu as pltpu
from jax.sharding import PartitionSpec as P

EPS_NORM = 1e-06
EPS_WHITE = 1e-08
CLIP = 0.2

HEAD_ROWS = 40
TOKEN_ROWS = 5
WIDTH = 16
OFFSET, SLOPE, COUNT, MEAN_L, MEAN_C, VAR_L, COV, VAR_C, LAST_DONE = range(9)

CONTRACT_LANES = (((1,), (1,)), ((), ()))


def column(ref, shape):
    row = lax.broadcasted_iota(jnp.int32, shape, 0)
    out = jnp.full(shape, ref[0], jnp.float32)
    for r in range(1, shape[0]):
        out = jnp.where(row == r, ref[r], out)
    return out


def lane_sum(x):
    return jnp.sum(x, axis=1, keepdims=True)


def head_kernel(
    gain_hbm,
    weight_hbm,
    done_hbm,
    mask_hbm,
    new_hbm,
    old_hbm,
    discount_hbm,
    trace_hbm,
    bootstrap_hbm,
    hidden_ref,
    out_ref,
    gate_ref,
    chain_ref,
    coef_ref,
    power_ref,
    fixed_ref,
    trace_ref,
    ratio_ref,
    start_ref,
    held,
    gain_ref,
    weight_ref,
    done_ref,
    mask_ref,
    new_ref,
    old_ref,
    discount_smem,
    trace_smem,
    bootstrap_smem,
    arrived,
):
    rollouts, length, width = held.shape
    peers = out_ref.shape[0] // HEAD_ROWS
    small = [
        pltpu.make_async_copy(source, target, arrived.at[rollouts + i])
        for i, (source, target) in enumerate(
            (
                (gain_hbm, gain_ref),
                (weight_hbm, weight_ref),
                (done_hbm, done_ref),
                (mask_hbm, mask_ref),
                (new_hbm, new_ref),
                (old_hbm, old_ref),
                (discount_hbm, discount_smem),
                (trace_hbm, trace_smem),
                (bootstrap_hbm, bootstrap_smem),
            )
        )
    ]
    copies = [
        pltpu.make_async_copy(hidden_ref.at[r], held.at[r], arrived.at[r]) for r in range(rollouts)
    ]
    for copy in small + copies:
        copy.start()
    for copy in small:
        copy.wait()

    shape = (rollouts, length)
    lane = lax.broadcasted_iota(jnp.int32, shape, 1)
    discount, trace = column(discount_smem, shape), column(trace_smem, shape)
    alive = 1.0 - done_ref[...].astype(jnp.float32)
    gate_ref[...] = discount * alive
    decay = discount * trace
    chain = decay * alive
    step, at = 1, 0
    while step < length:
        chain_ref[rollouts * at : rollouts * (at + 1), :] = chain
        later = pltpu.roll(chain, length - step, 1)
        chain = chain * jnp.where(lane < length - step, later, 1.0)
        step, at = 2 * step, at + 1
    coef_ref[...] = chain / trace
    left = length - 1 - lane
    power, factor, bit = discount, decay, 1
    while bit < length:
        power = jnp.where(left & bit != 0, power * factor, power)
        factor = factor * factor
        bit *= 2
    power_ref[...] = power
    last_done = jnp.max(
        jnp.where(alive > 0.5, -1.0, lane.astype(jnp.float32)), axis=1, keepdims=True
    )
    small_lane = lax.broadcasted_iota(jnp.int32, (rollouts, 128), 1)
    fixed = jnp.where(small_lane == SLOPE, chain[:, 0:1], 0.0)
    fixed_ref[...] = jnp.where(small_lane == LAST_DONE, last_done, fixed)
    trace_ref[...] = trace[:, :128]
    mask = mask_ref[...].astype(jnp.float32)
    ratio_ref[...] = mask * jnp.exp(new_ref[...] - old_ref[...])
    start_lane = lax.broadcasted_iota(jnp.int32, (1, 128), 1)
    start = jnp.full((1, 128), bootstrap_smem[0], jnp.float32)
    for r in range(1, rollouts):
        start = jnp.where(start_lane == WIDTH * r, bootstrap_smem[r], start)
    start_ref[...] = start

    scaled = gain_ref[...].astype(jnp.float32) * weight_ref[...].astype(jnp.float32)
    coarse = scaled.astype(jnp.bfloat16).astype(jnp.float32)
    fine = scaled - coarse
    row = lax.broadcasted_iota(jnp.int32, (8, 128), 0)
    tiles = []
    for j in range(width // 128):
        tile = jnp.where(row == 0, coarse[j : j + 1, :], 0.0)
        tiles.append(jnp.where(row == 1, fine[j : j + 1, :], tile))
    lhs = jnp.concatenate(tiles, axis=1).astype(jnp.bfloat16)
    ones = jnp.ones((8, 256), jnp.bfloat16)
    out_ref[32:33, :] = mask[:, :128]
    out_ref[33:34, :] = mask[:, 128:]
    out_ref[34:40, :] = jnp.zeros((6, 128), jnp.float32)
    for r in range(rollouts):
        copies[r].wait()
        block = held[r]
        products = lax.dot_general(lhs, block, CONTRACT_LANES, preferred_element_type=jnp.float32)
        products = products[0:1, :] + products[1:2, :]
        total = jnp.zeros((length, 128), jnp.float32)
        for j in range(width // 128):
            wide = held[r, :, 128 * j : 128 * (j + 1)].astype(jnp.float32)
            total = total + wide * wide
        high = total.astype(jnp.bfloat16)
        low = (total - high.astype(jnp.float32)).astype(jnp.bfloat16)
        squares = lax.dot_general(
            ones,
            jnp.concatenate([high, low], axis=1),
            CONTRACT_LANES,
            preferred_element_type=jnp.float32,
        )
        out_ref[r : r + 1, :] = squares[0:1, :128]
        out_ref[8 + r : 9 + r, :] = squares[0:1, 128:]
        out_ref[16 + r : 17 + r, :] = products[:, :128]
        out_ref[24 + r : 25 + r, :] = products[:, 128:]
    own = out_ref[0:HEAD_ROWS, :]
    for peer in range(1, peers):
        out_ref[HEAD_ROWS * peer : HEAD_ROWS * (peer + 1), :] = own


def local_kernel(
    hidden_width,
    recv_ref,
    rewards_ref,
    gate_ref,
    chain_ref,
    coef_ref,
    fixed_ref,
    trace_ref,
    ratio_ref,
    values_ref,
    out_ref,
):
    me = lax.axis_index("tensor")
    rollouts, length = rewards_ref.shape
    peers = recv_ref.shape[0] // HEAD_ROWS
    shape = (rollouts, length)
    total = recv_ref[0:32, :]
    for peer in range(1, peers):
        total = total + recv_ref[HEAD_ROWS * peer : HEAD_ROWS * peer + 32, :]
    squares = jnp.concatenate([total[0:8], total[8:16]], axis=1)
    products = jnp.concatenate([total[16:24], total[24:32]], axis=1)
    weight = jnp.concatenate(
        [
            recv_ref[pl.ds(32, peers, stride=HEAD_ROWS), :],
            recv_ref[pl.ds(33, peers, stride=HEAD_ROWS), :],
        ],
        axis=1,
    )
    values = products * lax.rsqrt(squares / hidden_width + EPS_NORM)
    lane = lax.broadcasted_iota(jnp.int32, shape, 1)
    inner_next = jnp.where(lane < length - 1, pltpu.roll(values, length - 1, 1), 0.0)
    local = rewards_ref[...] + gate_ref[...] * inner_next - values
    step, at = 1, 0
    while step < length:
        later = jnp.where(lane < length - step, pltpu.roll(local, length - step, 1), 0.0)
        local = local + chain_ref[rollouts * at : rollouts * (at + 1), :] * later
        step, at = 2 * step, at + 1
    coef = coef_ref[...]
    count = lane_sum(weight)
    safe = 1.0 / jnp.maximum(count, 1.0)
    mean_l = lane_sum(weight * local) * safe
    mean_c = lane_sum(weight * coef) * safe
    off_l = weight * (local - mean_l)
    off_c = weight * (coef - mean_c)
    stats = {
        OFFSET: values[:, 0:1] + trace_ref[:, 0:1] * local[:, 0:1],
        COUNT: count,
        MEAN_L: mean_l,
        MEAN_C: mean_c,
        VAR_L: lane_sum(off_l * off_l),
        COV: lane_sum(off_l * off_c),
        VAR_C: lane_sum(off_c * off_c),
    }
    small_lane = lax.broadcasted_iota(jnp.int32, (rollouts, 128), 1)
    summary = fixed_ref[...]
    for at, stat in stats.items():
        summary = jnp.where(small_lane == at, stat, summary)
    summary = pltpu.roll(summary, 0, 1, stride=WIDTH, stride_axis=0)
    summary = jnp.sum(summary, axis=0, keepdims=True)
    mine = lax.broadcasted_iota(jnp.int32, shape, 0) == me
    own_local = jnp.sum(jnp.where(mine, local, 0.0), axis=0, keepdims=True)
    values_ref[...] = jnp.sum(jnp.where(mine, values, 0.0), axis=0, keepdims=True)
    row = lax.broadcasted_iota(jnp.int32, (8, 128), 0)
    message = jnp.where(row == 0, summary, 0.0)
    message = jnp.where(row == 1, own_local[:, :128], message)
    message = jnp.where(row == 2, own_local[:, 128:], message)
    message = jnp.where(row == 3, ratio_ref[:, :128], message)
    message = jnp.where(row == 4, ratio_ref[:, 128:], message)
    for peer in range(out_ref.shape[0] // TOKEN_ROWS):
        out_ref[TOKEN_ROWS * peer : TOKEN_ROWS * (peer + 1), :] = message[0:TOKEN_ROWS, :]


def full_sum(x):
    return jnp.sum(jnp.sum(x, axis=0, keepdims=True), axis=1, keepdims=True)


def final_kernel(
    recv_ref,
    power_ref,
    start_ref,
    values_ref,
    values_hbm,
    white_hbm,
    loss_hbm,
    out_ref,
    white_ref,
    loss_ref,
    sent,
):
    tensor, seq = lax.axis_index("tensor"), lax.axis_index("seq")
    writes = [
        pltpu.make_async_copy(source, target, sent.at[i])
        for i, (source, target) in enumerate(
            ((values_ref, values_hbm), (white_ref, white_hbm), (loss_ref, loss_hbm))
        )
    ]
    writes[0].start()
    blocks = recv_ref.shape[0] // TOKEN_ROWS
    rollouts = out_ref.shape[0]
    shape = (blocks, 128)
    table = recv_ref[pl.ds(0, blocks, stride=TOKEN_ROWS), :]
    row = lax.broadcasted_iota(jnp.int32, shape, 0)
    lane = lax.broadcasted_iota(jnp.int32, shape, 1)

    def stat(at):
        return pltpu.roll(table, 128 - at, 1)

    last = row == blocks - 1
    offset = jnp.where(last, start_ref[...], pltpu.roll(table, blocks - 1, 0))
    slope = jnp.where(last, 0.0, pltpu.roll(stat(SLOPE), blocks - 1, 0))
    step = 1
    while step < blocks:
        inside = row < blocks - step
        offset_later = jnp.where(inside, pltpu.roll(offset, blocks - step, 0), 0.0)
        slope_later = jnp.where(inside, pltpu.roll(slope, blocks - step, 0), 0.0)
        offset = offset + slope * offset_later
        slope = slope * slope_later
        step *= 2
    entering = offset
    used = (lane % WIDTH == 0) & (lane < WIDTH * rollouts)
    members = jnp.where(used, stat(COUNT), 0.0)
    block_mean = jnp.where(used, stat(MEAN_L) + entering * stat(MEAN_C), 0.0)
    count = full_sum(members)
    mean = full_sum(members * block_mean) / count
    within = stat(VAR_L) + entering * (2.0 * stat(COV) + entering * stat(VAR_C))
    apart = block_mean - mean
    variance = full_sum(jnp.where(used, within, 0.0) + members * apart * apart) / count
    scale = lax.rsqrt(variance + EPS_WHITE)

    mine = lane == WIDTH * tensor
    own_entering = lane_sum(jnp.where(mine, entering, 0.0))
    own_done = lane_sum(jnp.where(mine, stat(LAST_DONE), 0.0))
    power = power_ref[pl.ds(tensor, 1), :]
    loss = jnp.zeros(shape, jnp.float32)
    mine_row = row == seq
    for half in range(2):
        lanes = slice(128 * half, 128 * (half + 1))
        position = (lane + 128 * half).astype(jnp.float32)
        coef = jnp.where(position > own_done, power[:, lanes], 0.0)
        local = recv_ref[pl.ds(1 + half, blocks, stride=TOKEN_ROWS), :]
        ratio = recv_ref[pl.ds(3 + half, blocks, stride=TOKEN_ROWS), :]
        white = (local + coef * own_entering - mean) * scale
        clipped = jnp.clip(ratio, 1.0 - CLIP, 1.0 + CLIP)
        token = jnp.where(ratio > 0.0, -jnp.minimum(ratio * white, clipped * white), 0.0)
        loss = loss + token
        white_ref[:, lanes] = jnp.sum(jnp.where(mine_row, white, 0.0), axis=0, keepdims=True)
        loss_ref[:, lanes] = jnp.sum(jnp.where(mine_row, token, 0.0), axis=0, keepdims=True)
    writes[1].start()
    writes[2].start()
    out_ref[...] = jnp.broadcast_to(full_sum(loss) / count, out_ref.shape)
    for write in writes:
        write.wait()


VMEM = pl.BlockSpec(memory_space=pltpu.VMEM)
ANY = pl.BlockSpec(memory_space=pl.ANY)


def on_chip(x):
    return pltpu.with_memory_space_constraint(x, pltpu.VMEM)


def on_chip_shape(shape):
    return pltpu.VMEM(shape, jnp.float32)


def exchange(x, axis):
    return lax.all_to_all(x, axis, 0, 0, tiled=True)


def shards(
    hidden,
    norm_gain,
    value_weight,
    rewards,
    done_flags,
    valid_mask,
    new_logprob,
    old_logprob,
    discount,
    trace_decay,
    bootstrap,
):
    rollouts, length, width = hidden.shape
    peers, blocks = lax.axis_size("tensor"), lax.axis_size("seq")
    f32 = jnp.float32
    steps = length.bit_length() - 1
    sent, gate, chain, coef, power, fixed, trace, ratio, start = pl.pallas_call(
        head_kernel,
        out_shape=(
            on_chip_shape((peers * HEAD_ROWS, 128)),
            on_chip_shape((rollouts, length)),
            on_chip_shape((rollouts * steps, length)),
            on_chip_shape((rollouts, length)),
            on_chip_shape((rollouts, length)),
            on_chip_shape((rollouts, 128)),
            on_chip_shape((rollouts, 128)),
            on_chip_shape((1, length)),
            on_chip_shape((1, 128)),
        ),
        in_specs=[ANY] * 10,
        out_specs=(VMEM,) * 9,
        scratch_shapes=[
            pltpu.VMEM(hidden.shape, hidden.dtype),
            pltpu.VMEM((width // 128, 128), norm_gain.dtype),
            pltpu.VMEM((width // 128, 128), value_weight.dtype),
            pltpu.VMEM(done_flags.shape, done_flags.dtype),
            pltpu.VMEM(valid_mask.shape, valid_mask.dtype),
            pltpu.VMEM(new_logprob.shape, f32),
            pltpu.VMEM(old_logprob.shape, f32),
            pltpu.SMEM(discount.shape, f32),
            pltpu.SMEM(trace_decay.shape, f32),
            pltpu.SMEM(bootstrap.shape, f32),
            pltpu.SemaphoreType.DMA((rollouts + 9,)),
        ],
        name="head",
    )(
        norm_gain.reshape(-1, 128),
        value_weight.reshape(-1, 128),
        done_flags,
        valid_mask,
        new_logprob,
        old_logprob,
        discount,
        trace_decay,
        bootstrap,
        hidden,
    )
    got = exchange(sent.reshape(peers, 1, HEAD_ROWS * 128), "tensor")
    values, sent = pl.pallas_call(
        lambda *refs: local_kernel(width * peers, *refs),
        out_shape=(
            on_chip_shape((1, length)),
            on_chip_shape((blocks * TOKEN_ROWS, 128)),
        ),
        in_specs=[VMEM] * 8,
        out_specs=(VMEM, VMEM),
        name="local",
    )(
        *map(
            on_chip,
            (
                got.reshape(peers * HEAD_ROWS, 128),
                rewards,
                gate,
                chain,
                coef,
                fixed,
                trace,
                ratio,
            ),
        )
    )
    got = exchange(sent.reshape(blocks, 1, TOKEN_ROWS * 128), "seq")
    own_row = jax.ShapeDtypeStruct((1, length), f32)
    values, white, loss, sent = pl.pallas_call(
        final_kernel,
        out_shape=(own_row, own_row, own_row, on_chip_shape((peers, 128))),
        in_specs=[VMEM] * 4,
        out_specs=(ANY, ANY, ANY, VMEM),
        scratch_shapes=[
            pltpu.VMEM((1, length), f32),
            pltpu.VMEM((1, length), f32),
            pltpu.SemaphoreType.DMA((3,)),
        ],
        name="final",
    )(*map(on_chip, (got.reshape(blocks * TOKEN_ROWS, 128), power, start, values)))
    got = exchange(sent.reshape(peers, 1, 128), "tensor")
    return values, white, loss, jnp.sum(got[:, 0, 0])


def solution(mesh):
    in_specs = (
        P(None, "seq", "tensor"),
        P("tensor"),
        P("tensor"),
        P(None, "seq"),
        P(None, "seq"),
        P("tensor", "seq"),
        P("tensor", "seq"),
        P("tensor", "seq"),
        P(),
        P(),
        P(),
    )
    out_specs = (P("tensor", "seq"), P("tensor", "seq"), P("tensor", "seq"), P())
    return jax.shard_map(
        shards, mesh=mesh, in_specs=in_specs, out_specs=out_specs, check_vma=False
    )
```

time: 67.4 us -> 62.2 us (0.923)
  Pallas kernels: 9.99 us -> 6.44 us
  blocking collectives: 55.8 us -> 54.3 us
    pallas_call x2, Pallas kernels: 7.52 us -> 5.6 us  [the longest x1 4.67 us: shards(): pl.pallas_call(head_kernel, out_shape=(on_chip_shape((peers * HEAD_ROWS,...]
    pallas_call x1, Pallas kernels: 2.47 us -> 0.84 us  [shards(): pl.pallas_call(lambda *refs: local_kernel(width * peers, *refs), out_shap...]
    all_to_all x3, blocking collectives: 55.8 us -> 54.3 us  [exchange(): return lax.all_to_all(x, axis, 0, 0, tiled=True)]
where the time goes in v2:
time: 62.2 us; the launch traced here: 62 us
  blocking collectives  54.3 us (87%)
  Pallas kernels  6.44 us (10%)
  between operations  0.67 us (1%)
    all_to_all x3, blocking collectives, exchange(): return lax.all_to_all(x, axis, 0, 0, tiled=True)  54.3 us
    pallas_call x1, Pallas kernels, shards(): pl.pallas_call(head_kernel, out_shape=(on_chip_shape((peers * HEAD_ROWS,...  4.67 us

profile of v2, /device:TPU:1, one launch (start us, length us, event | category | flops | bytes accessed | tf_op | source)
XLA Modules:
  0.0 62.0 jit_solution(16475221409509739211)
XLA Ops:
  0.6 0.0 copy-start
  0.6 4.7 %head.1 = (f32[320,128]{1,0:T(8,128)S(1)}, f32[8,256]{1,0:T(8,128)S(1)}, f32[64,256]{1,0:T(8,128)S(1)}, f32[8,256]{1,0:T(8,128)S(1)}, f32[8,256]{1,0:T(8,128)S(1...) custom-call(bf16[8,128]{1,0:T(8,128)(2,1)} %bitcast.14, ...), custom_call_target="tpu_custom_call" | custom-call | tf_op jit(solution)/shard_map/head/pallas_call | solution.py:353
  5.3 14.8 %all_to_all.15 = f32[8,1,5120]{2,1,0:T(1,128)S(1)} all-to-all(f32[8,1,5120]{2,1,0:T(1,128)S(1)} %bitcast.11), channel_id=1, replica_groups=mesh['seq'=64,'tensor'=8] {'tensor'}, dimensions={0} | all-to-all | bytes 327680 | tf_op jit(solution)/shard_map/all_to_all | solution.py:333
  20.1 0.0 copy-done
  20.1 0.8 %local.1 = (f32[1,256]{1,0:T(1,128)S(1)}, f32[320,128]{1,0:T(8,128)S(1)}) custom-call(f32[320,128]{1,0:T(8,128)S(1)} %bitcast.10, f32[8,256]{1,0:T(8,128)S(1)} %copy-done, f32[8,256]{1,0:T(8,128)S(1)} %get-tuple-element.20.refs_2_, f32[64,256]{1,0:T(8,128)S(1)} %get-tuple-element.21.refs_3_, f32[8,256]{1,0:T(8,128)S(1)} %get-tuple-element.22.refs_4_, ...), custom_call_target="tpu_custom_call" | custom-call | tf_op jit(solution)/shard_map/local/pallas_call | solution.py:395
  21.0 29.7 %all_to_all.16 = f32[64,1,640]{2,1,0:T(1,128)S(1)} all-to-all(f32[64,1,640]{2,1,0:T(1,128)S(1)} %bitcast.12), channel_id=1, replica_groups=mesh['seq'=64,'tensor'=8] {'seq'}, dimensions={0} | all-to-all | bytes 327680 | tf_op jit(solution)/shard_map/all_to_all | solution.py:333
  50.6 0.9 %final.1 = (f32[1,256]{1,0:T(1,128)}, f32[1,256]{1,0:T(1,128)}, f32[1,256]{1,0:T(1,128)}, f32[8,128]{1,0:T(8,128)S(1)}) custom-call(f32[320,128]{1,0:T(8,128)S(1)} %bitcast.9, f32[8,256]{1,0:T(8,128)S(1)} %get-tuple-element.27.power_ref, f32[1,128]{1,0:T(1,128)S(1)} %get-tuple-element.28.start_ref, f32[1,256]{1,0:T(1,128)S(1)} %get-tuple-element.29.values_ref), custom_call_target="tpu_custom_call" | custom-call | tf_op jit(solution)/shard_map/final/pallas_call | solution.py:421
  51.6 9.9 %all_to_all.17 = f32[8,1,128]{2,1,0:T(1,128)S(1)} all-to-all(f32[8,1,128]{2,1,0:T(1,128)S(1)} %bitcast.13), channel_id=1, replica_groups=mesh['seq'=64,'tensor'=8] {'tensor'}, dimensions={0} | all-to-all | bytes 8192 | tf_op jit(solution)/shard_map/all_to_all | solution.py:333
  61.4 0.6 slice_reduce_fusion
Async XLA Ops:
  0.6 19.5 %copy-start = (f32[8,256]{1,0:T(8,128)S(1)}, f32[8,256]{1,0:T(8,128)}, u32[]{:S(2)}) copy-start(f32[8,256]{1,0:T(8,128)} %refs_1_.1) | copy-start | bytes 24580

commit v3 on v2

--- a/solution.py
+++ b/solution.py
@@ -1,3 +1,5 @@
+from functools import partial
+
 import jax
 import jax.numpy as jnp
 from jax import lax
@@ -13,6 +15,8 @@
 TOKEN_ROWS = 5
 WIDTH = 16
 OFFSET, SLOPE, COUNT, MEAN_L, MEAN_C, VAR_L, COV, VAR_C, LAST_DONE = range(9)
+
+CHUNK = 64
 
 CONTRACT_LANES = (((1,), (1,)), ((), ()))
 
@@ -59,6 +63,7 @@
     discount_smem,
     trace_smem,
     bootstrap_smem,
+    fold_ref,
     arrived,
 ):
     rollouts, length, width = held.shape
@@ -82,84 +87,124 @@
     copies = [
         pltpu.make_async_copy(hidden_ref.at[r], held.at[r], arrived.at[r]) for r in range(rollouts)
     ]
-    for copy in small + copies:
+    for copy in copies[:1] + small + copies[1:]:
         copy.start()
     for copy in small:
         copy.wait()
 
+    scaled = gain_ref[...].astype(jnp.float32) * weight_ref[...].astype(jnp.float32)
+    small_lane = lax.broadcasted_iota(jnp.int32, (8, 128), 1)
+    levels = rollouts.bit_length() - 1
+    group = 64 >> levels
+
+    def fold(even, odd, distance):
+        even = even + pltpu.roll(even, 128 - distance, 1)
+        odd = odd + pltpu.roll(odd, distance, 1)
+        return jnp.where((small_lane[0:1] // distance) % 2 == 0, even, odd)
+
+    def partial_sums(r, here):
+        squares = products = jnp.zeros((CHUNK, 128), jnp.float32)
+        for j in range(width // 128):
+            wide = held[r, here, 128 * j : 128 * (j + 1)].astype(jnp.float32)
+            squares = squares + wide * wide
+            products = products + wide * scaled[j : j + 1, :]
+        folded, distance = fold(squares, products, 64), 32
+        for level in range(levels):
+            if not (r >> level) & 1:
+                fold_ref[level, here] = folded
+                return None
+            folded, distance = fold(fold_ref[level, here], folded, distance), distance // 2
+        return folded
+
+    def finish(half, folded):
+        turned = jnp.transpose(folded)
+        sublane = lax.broadcasted_iota(jnp.int32, (8, 128), 0)
+        for kind in range(2):
+            rows = []
+            for r in range(rollouts):
+                at = kind
+                for level in range(levels):
+                    at = 2 * at + (r >> level) % 2
+                rows.append(turned[group * at : group * (at + 1)])
+            distance = group // 2
+            while distance:
+                even, odd = rows[:distance], rows[distance:]
+                rows = []
+                for e, o in zip(even, odd, strict=True):
+                    e = e + pltpu.roll(e, 8 - distance, 0)
+                    o = o + pltpu.roll(o, distance, 0)
+                    rows.append(jnp.where((sublane // distance) % 2 == 0, e, o))
+                distance //= 2
+            for peer in range(peers):
+                at = HEAD_ROWS * peer + 8 * (2 * kind + half)
+                out_ref[at : at + 8, :] = rows[0]
+
     shape = (rollouts, length)
     lane = lax.broadcasted_iota(jnp.int32, shape, 1)
-    discount, trace = column(discount_smem, shape), column(trace_smem, shape)
-    alive = 1.0 - done_ref[...].astype(jnp.float32)
-    gate_ref[...] = discount * alive
-    decay = discount * trace
-    chain = decay * alive
-    step, at = 1, 0
-    while step < length:
-        chain_ref[rollouts * at : rollouts * (at + 1), :] = chain
+
+    def piece_own():
+        mask = mask_ref[...].astype(jnp.float32)
+        ratio_ref[...] = mask * jnp.exp(new_ref[...] - old_ref[...])
+        row = lax.broadcasted_iota(jnp.int32, (8, 128), 0)
+        rest = jnp.where(row == 0, mask[:, :128], jnp.where(row == 1, mask[:, 128:], 0.0))
+        for peer in range(peers):
+            out_ref[HEAD_ROWS * peer + 32 : HEAD_ROWS * (peer + 1), :] = rest
+        start_lane = lax.broadcasted_iota(jnp.int32, (1, 128), 1)
+        start = jnp.full((1, 128), bootstrap_smem[0], jnp.float32)
+        for r in range(1, rollouts):
+            start = jnp.where(start_lane == WIDTH * r, bootstrap_smem[r], start)
+        start_ref[...] = start
+
+    def piece_chain_start():
+        discount, trace = column(discount_smem, shape), column(trace_smem, shape)
+        alive = 1.0 - done_ref[...].astype(jnp.float32)
+        gate_ref[...] = discount * alive
+        chain_ref[0:rollouts, :] = discount * trace * alive
+        trace_ref[...] = trace[:, :128]
+        last_done = jnp.where(alive > 0.5, -1.0, lane.astype(jnp.float32))
+        last_done = jnp.max(last_done, axis=1, keepdims=True)
+        fixed_ref[...] = jnp.where(small_lane == LAST_DONE, last_done, 0.0)
+
+    def piece_chain(at):
+        step = 1 << at
+        chain = chain_ref[rollouts * at : rollouts * (at + 1), :]
         later = pltpu.roll(chain, length - step, 1)
         chain = chain * jnp.where(lane < length - step, later, 1.0)
-        step, at = 2 * step, at + 1
-    coef_ref[...] = chain / trace
-    left = length - 1 - lane
-    power, factor, bit = discount, decay, 1
-    while bit < length:
-        power = jnp.where(left & bit != 0, power * factor, power)
-        factor = factor * factor
-        bit *= 2
-    power_ref[...] = power
-    last_done = jnp.max(
-        jnp.where(alive > 0.5, -1.0, lane.astype(jnp.float32)), axis=1, keepdims=True
-    )
-    small_lane = lax.broadcasted_iota(jnp.int32, (rollouts, 128), 1)
-    fixed = jnp.where(small_lane == SLOPE, chain[:, 0:1], 0.0)
-    fixed_ref[...] = jnp.where(small_lane == LAST_DONE, last_done, fixed)
-    trace_ref[...] = trace[:, :128]
-    mask = mask_ref[...].astype(jnp.float32)
-    ratio_ref[...] = mask * jnp.exp(new_ref[...] - old_ref[...])
-    start_lane = lax.broadcasted_iota(jnp.int32, (1, 128), 1)
-    start = jnp.full((1, 128), bootstrap_smem[0], jnp.float32)
-    for r in range(1, rollouts):
-        start = jnp.where(start_lane == WIDTH * r, bootstrap_smem[r], start)
-    start_ref[...] = start
-
-    scaled = gain_ref[...].astype(jnp.float32) * weight_ref[...].astype(jnp.float32)
-    coarse = scaled.astype(jnp.bfloat16).astype(jnp.float32)
-    fine = scaled - coarse
-    row = lax.broadcasted_iota(jnp.int32, (8, 128), 0)
-    tiles = []
-    for j in range(width // 128):
-        tile = jnp.where(row == 0, coarse[j : j + 1, :], 0.0)
-        tiles.append(jnp.where(row == 1, fine[j : j + 1, :], tile))
-    lhs = jnp.concatenate(tiles, axis=1).astype(jnp.bfloat16)
-    ones = jnp.ones((8, 256), jnp.bfloat16)
-    out_ref[32:33, :] = mask[:, :128]
-    out_ref[33:34, :] = mask[:, 128:]
-    out_ref[34:40, :] = jnp.zeros((6, 128), jnp.float32)
+        if 2 * step < length:
+            chain_ref[rollouts * (at + 1) : rollouts * (at + 2), :] = chain
+            return
+        coef_ref[...] = chain / column(trace_smem, shape)
+        fixed_ref[...] = jnp.where(small_lane == SLOPE, chain[:, 0:1], fixed_ref[...])
+
+    def piece_power():
+        discount = column(discount_smem, shape)
+        left = length - 1 - lane
+        power, factor, bit = discount, discount * column(trace_smem, shape), 1
+        while bit < length:
+            power = jnp.where(left & bit != 0, power * factor, power)
+            factor = factor * factor
+            bit *= 2
+        power_ref[...] = power
+
+    steps = length.bit_length() - 1
+    pieces = [[] for _ in range(rollouts)]
+    pieces[0] = [piece_chain_start]
+    for at in range(steps):
+        pieces[1 + at * (rollouts - 2) // steps].append(partial(piece_chain, at))
+    pieces[0].append(piece_own)
+    pieces[rollouts - 2].append(piece_power)
+
     for r in range(rollouts):
         copies[r].wait()
-        block = held[r]
-        products = lax.dot_general(lhs, block, CONTRACT_LANES, preferred_element_type=jnp.float32)
-        products = products[0:1, :] + products[1:2, :]
-        total = jnp.zeros((length, 128), jnp.float32)
-        for j in range(width // 128):
-            wide = held[r, :, 128 * j : 128 * (j + 1)].astype(jnp.float32)
-            total = total + wide * wide
-        high = total.astype(jnp.bfloat16)
-        low = (total - high.astype(jnp.float32)).astype(jnp.bfloat16)
-        squares = lax.dot_general(
-            ones,
-            jnp.concatenate([high, low], axis=1),
-            CONTRACT_LANES,
-            preferred_element_type=jnp.float32,
-        )
-        out_ref[r : r + 1, :] = squares[0:1, :128]
-        out_ref[8 + r : 9 + r, :] = squares[0:1, 128:]
-        out_ref[16 + r : 17 + r, :] = products[:, :128]
-        out_ref[24 + r : 25 + r, :] = products[:, 128:]
-    own = out_ref[0:HEAD_ROWS, :]
-    for peer in range(1, peers):
-        out_ref[HEAD_ROWS * peer : HEAD_ROWS * (peer + 1), :] = own
+        for piece in pieces[r]:
+            piece()
+        for half in range(2):
+            folded = [
+                partial_sums(r, slice(first, first + CHUNK))
+                for first in range(128 * half, 128 * (half + 1), CHUNK)
+            ]
+            if r == rollouts - 1:
+                finish(half, jnp.concatenate(folded, axis=0))
 
 
 def local_kernel(
@@ -333,11 +378,11 @@
     return lax.all_to_all(x, axis, 0, 0, tiled=True)
 
 
-def shards(
+def run_head(
+    peers,
     hidden,
     norm_gain,
     value_weight,
-    rewards,
     done_flags,
     valid_mask,
     new_logprob,
@@ -347,10 +392,9 @@
     bootstrap,
 ):
     rollouts, length, width = hidden.shape
-    peers, blocks = lax.axis_size("tensor"), lax.axis_size("seq")
     f32 = jnp.float32
     steps = length.bit_length() - 1
-    sent, gate, chain, coef, power, fixed, trace, ratio, start = pl.pallas_call(
+    return pl.pallas_call(
         head_kernel,
         out_shape=(
             on_chip_shape((peers * HEAD_ROWS, 128)),
@@ -376,6 +420,7 @@
             pltpu.SMEM(discount.shape, f32),
             pltpu.SMEM(trace_decay.shape, f32),
             pltpu.SMEM(bootstrap.shape, f32),
+            pltpu.VMEM((3, length, 128), f32),
             pltpu.SemaphoreType.DMA((rollouts + 9,)),
         ],
         name="head",
@@ -390,6 +435,36 @@
         trace_decay,
         bootstrap,
         hidden,
+    )
+
+
+def shards(
+    hidden,
+    norm_gain,
+    value_weight,
+    rewards,
+    done_flags,
+    valid_mask,
+    new_logprob,
+    old_logprob,
+    discount,
+    trace_decay,
+    bootstrap,
+):
+    rollouts, length, width = hidden.shape
+    peers, blocks = lax.axis_size("tensor"), lax.axis_size("seq")
+    sent, gate, chain, coef, power, fixed, trace, ratio, start = run_head(
+        peers,
+        hidden,
+        norm_gain,
+        value_weight,
+        done_flags,
+        valid_mask,
+        new_logprob,
+        old_logprob,
+        discount,
+        trace_decay,
+        bootstrap,
     )
     got = exchange(sent.reshape(peers, 1, HEAD_ROWS * 128), "tensor")
     values, sent = pl.pallas_call(
@@ -417,15 +492,15 @@
         )
     )
     got = exchange(sent.reshape(blocks, 1, TOKEN_ROWS * 128), "seq")
-    own_row = jax.ShapeDtypeStruct((1, length), f32)
+    own_row = jax.ShapeDtypeStruct((1, length), jnp.float32)
     values, white, loss, sent = pl.pallas_call(
         final_kernel,
         out_shape=(own_row, own_row, own_row, on_chip_shape((peers, 128))),
         in_specs=[VMEM] * 4,
         out_specs=(ANY, ANY, ANY, VMEM),
         scratch_shapes=[
-            pltpu.VMEM((1, length), f32),
-            pltpu.VMEM((1, length), f32),
+            pltpu.VMEM((1, length), jnp.float32),
+            pltpu.VMEM((1, length), jnp.float32),
             pltpu.SemaphoreType.DMA((3,)),
         ],
         name="final",

time: 62.2 us -> 61.4 us (0.987)
  Pallas kernels: 6.44 us -> 5.59 us
    pallas_call x1, Pallas kernels: 4.67 us -> 3.83 us  [run_head(): pl.pallas_call(head_kernel, out_shape=(on_chip_shape((peers * HEAD_ROWS,...]
where the time goes in v3:
time: 61.4 us; the launch traced here: 61.2 us
  blocking collectives  54.3 us (88%)
  Pallas kernels  5.59 us (9%)
  between operations  0.67 us (1%)
    all_to_all x3, blocking collectives, exchange(): return lax.all_to_all(x, axis, 0, 0, tiled=True)  54.3 us
    pallas_call x1, Pallas kernels, run_head(): pl.pallas_call(head_kernel, out_shape=(on_chip_shape((peers * HEAD_ROWS,...  3.83 us

profile of v3, /device:TPU:1, one launch (start us, length us, event | category | flops | bytes accessed | tf_op | source)
XLA Modules:
  0.0 61.2 jit_solution(6711134096509786811)
XLA Ops:
  0.6 0.0 copy-start
  0.6 3.8 %head.1 = (f32[320,128]{1,0:T(8,128)S(1)}, f32[8,256]{1,0:T(8,128)S(1)}, f32[64,256]{1,0:T(8,128)S(1)}, f32[8,256]{1,0:T(8,128)S(1)}, f32[8,256]{1,0:T(8,128)S(1...) custom-call(bf16[8,128]{1,0:T(8,128)(2,1)} %bitcast.14, ...), custom_call_target="tpu_custom_call" | custom-call | tf_op jit(solution)/shard_map/head/pallas_call | solution.py:397
  4.5 14.8 %all_to_all.15 = f32[8,1,5120]{2,1,0:T(1,128)S(1)} all-to-all(f32[8,1,5120]{2,1,0:T(1,128)S(1)} %bitcast.11), channel_id=1, replica_groups=mesh['seq'=64,'tensor'=8] {'tensor'}, dimensions={0} | all-to-all | bytes 327680 | tf_op jit(solution)/shard_map/all_to_all | solution.py:378
  19.3 0.0 copy-done
  19.3 0.8 %local.1 = (f32[1,256]{1,0:T(1,128)S(1)}, f32[320,128]{1,0:T(8,128)S(1)}) custom-call(f32[320,128]{1,0:T(8,128)S(1)} %bitcast.10, f32[8,256]{1,0:T(8,128)S(1)} %copy-done, f32[8,256]{1,0:T(8,128)S(1)} %get-tuple-element.20.refs_2_, f32[64,256]{1,0:T(8,128)S(1)} %get-tuple-element.21.refs_3_, f32[8,256]{1,0:T(8,128)S(1)} %get-tuple-element.22.refs_4_, ...), custom_call_target="tpu_custom_call" | custom-call | tf_op jit(solution)/shard_map/local/pallas_call | solution.py:470
  20.1 29.7 %all_to_all.16 = f32[64,1,640]{2,1,0:T(1,128)S(1)} all-to-all(f32[64,1,640]{2,1,0:T(1,128)S(1)} %bitcast.12), channel_id=1, replica_groups=mesh['seq'=64,'tensor'=8] {'seq'}, dimensions={0} | all-to-all | bytes 327680 | tf_op jit(solution)/shard_map/all_to_all | solution.py:378
  49.8 0.9 %final.1 = (f32[1,256]{1,0:T(1,128)}, f32[1,256]{1,0:T(1,128)}, f32[1,256]{1,0:T(1,128)}, f32[8,128]{1,0:T(8,128)S(1)}) custom-call(f32[320,128]{1,0:T(8,128)S(1)} %bitcast.9, f32[8,256]{1,0:T(8,128)S(1)} %get-tuple-element.27.power_ref, f32[1,128]{1,0:T(1,128)S(1)} %get-tuple-element.28.start_ref, f32[1,256]{1,0:T(1,128)S(1)} %get-tuple-element.29.values_ref), custom_call_target="tpu_custom_call" | custom-call | tf_op jit(solution)/shard_map/final/pallas_call | solution.py:496
  50.7 9.9 %all_to_all.17 = f32[8,1,128]{2,1,0:T(1,128)S(1)} all-to-all(f32[8,1,128]{2,1,0:T(1,128)S(1)} %bitcast.13), channel_id=1, replica_groups=mesh['seq'=64,'tensor'=8] {'tensor'}, dimensions={0} | all-to-all | bytes 8192 | tf_op jit(solution)/shard_map/all_to_all | solution.py:378
  60.6 0.6 slice_reduce_fusion
Async XLA Ops:
  0.6 18.6 %copy-start = (f32[8,256]{1,0:T(8,128)S(1)}, f32[8,256]{1,0:T(8,128)}, u32[]{:S(2)}) copy-start(f32[8,256]{1,0:T(8,128)} %refs_1_.1) | copy-start | bytes 24580

commit v4 on v3

--- a/solution.py
+++ b/solution.py
@@ -280,11 +280,18 @@
         out_ref[TOKEN_ROWS * peer : TOKEN_ROWS * (peer + 1), :] = message[0:TOKEN_ROWS, :]
 
 
+def in_order(ref, at, first):
+    blocks = ref.shape[0] // TOKEN_ROWS
+    rows = ref[pl.ds(at, blocks, stride=TOKEN_ROWS), :]
+    return jnp.concatenate([rows[blocks - first :], rows[: blocks - first]], axis=0)
+
+
 def full_sum(x):
     return jnp.sum(jnp.sum(x, axis=0, keepdims=True), axis=1, keepdims=True)
 
 
 def final_kernel(
+    first,
     recv_ref,
     power_ref,
     start_ref,
@@ -308,7 +315,7 @@
     blocks = recv_ref.shape[0] // TOKEN_ROWS
     rollouts = out_ref.shape[0]
     shape = (blocks, 128)
-    table = recv_ref[pl.ds(0, blocks, stride=TOKEN_ROWS), :]
+    table = in_order(recv_ref, 0, first)
     row = lax.broadcasted_iota(jnp.int32, shape, 0)
     lane = lax.broadcasted_iota(jnp.int32, shape, 1)
 
@@ -347,8 +354,8 @@
         lanes = slice(128 * half, 128 * (half + 1))
         position = (lane + 128 * half).astype(jnp.float32)
         coef = jnp.where(position > own_done, power[:, lanes], 0.0)
-        local = recv_ref[pl.ds(1 + half, blocks, stride=TOKEN_ROWS), :]
-        ratio = recv_ref[pl.ds(3 + half, blocks, stride=TOKEN_ROWS), :]
+        local = in_order(recv_ref, 1 + half, first)
+        ratio = in_order(recv_ref, 3 + half, first)
         white = (local + coef * own_entering - mean) * scale
         clipped = jnp.clip(ratio, 1.0 - CLIP, 1.0 + CLIP)
         token = jnp.where(ratio > 0.0, -jnp.minimum(ratio * white, clipped * white), 0.0)
@@ -374,8 +381,10 @@
     return pltpu.VMEM(shape, jnp.float32)
 
 
-def exchange(x, axis):
-    return lax.all_to_all(x, axis, 0, 0, tiled=True)
+def exchange(x, axis, first=0):
+    size = lax.axis_size(axis)
+    order = [(first + i) % size for i in range(size)]
+    return lax.all_to_all(x, axis, 0, 0, axis_index_groups=[order], tiled=True)
 
 
 def run_head(
@@ -491,10 +500,11 @@
             ),
         )
     )
-    got = exchange(sent.reshape(blocks, 1, TOKEN_ROWS * 128), "seq")
+    first = blocks * 7 // 8
+    got = exchange(sent.reshape(blocks, 1, TOKEN_ROWS * 128), "seq", first)
     own_row = jax.ShapeDtypeStruct((1, length), jnp.float32)
     values, white, loss, sent = pl.pallas_call(
-        final_kernel,
+        partial(final_kernel, first),
         out_shape=(own_row, own_row, own_row, on_chip_shape((peers, 128))),
         in_specs=[VMEM] * 4,
         out_specs=(ANY, ANY, ANY, VMEM),

time: 61.4 us -> 56.8 us (0.925)
  blocking collectives: 54.3 us -> 49.8 us
    all_to_all x3, blocking collectives: 54.3 us -> 49.8 us  [exchange(): return lax.all_to_all(x, axis, 0, 0, axis_index_groups=[order], tiled=True)]
where the time goes in v4:
time: 56.8 us; the launch traced here: 56.6 us
  blocking collectives  49.8 us (88%)
  Pallas kernels  5.59 us (10%)
  between operations  0.67 us (1%)
  other arithmetic  0.61 us (1%)
    all_to_all x3, blocking collectives, exchange(): return lax.all_to_all(x, axis, 0, 0, axis_index_groups=[order], tiled=True)  49.8 us
    pallas_call x1, Pallas kernels, run_head(): pl.pallas_call(head_kernel, out_shape=(on_chip_shape((peers * HEAD_ROWS,...  3.83 us

profile of v4, /device:TPU:1, one launch (start us, length us, event | category | flops | bytes accessed | tf_op | source)
XLA Modules:
  0.0 56.6 jit_solution(7968022101733785816)
XLA Ops:
  0.6 0.0 copy-start
  0.6 3.8 %head.1 = (f32[320,128]{1,0:T(8,128)S(1)}, f32[8,256]{1,0:T(8,128)S(1)}, f32[64,256]{1,0:T(8,128)S(1)}, f32[8,256]{1,0:T(8,128)S(1)}, f32[8,256]{1,0:T(8,128)S(1...) custom-call(bf16[8,128]{1,0:T(8,128)(2,1)} %bitcast.14, ...), custom_call_target="tpu_custom_call" | custom-call | tf_op jit(solution)/shard_map/head/pallas_call | solution.py:406
  4.5 14.8 %all_to_all.15 = f32[8,1,5120]{2,1,0:T(1,128)S(1)} all-to-all(f32[8,1,5120]{2,1,0:T(1,128)S(1)} %bitcast.11), channel_id=1, replica_groups={{0,1,2,3,4,5,6,7},{8,9,10,11,12,13,14,15},{16,17,18,19,20,21,22,23},{24..., dimensions={0} | all-to-all | bytes 327680 | tf_op jit(solution)/shard_map/all_to_all | solution.py:387
  19.3 0.0 copy-done
  19.3 0.8 %local.1 = (f32[1,256]{1,0:T(1,128)S(1)}, f32[320,128]{1,0:T(8,128)S(1)}) custom-call(f32[320,128]{1,0:T(8,128)S(1)} %bitcast.10, f32[8,256]{1,0:T(8,128)S(1)} %copy-done, f32[8,256]{1,0:T(8,128)S(1)} %get-tuple-element.20.refs_2_, f32[64,256]{1,0:T(8,128)S(1)} %get-tuple-element.21.refs_3_, f32[8,256]{1,0:T(8,128)S(1)} %get-tuple-element.22.refs_4_, ...), custom_call_target="tpu_custom_call" | custom-call | tf_op jit(solution)/shard_map/local/pallas_call | solution.py:479
  20.1 26.1 %all_to_all.16 = f32[64,1,640]{2,1,0:T(1,128)S(1)} all-to-all(f32[64,1,640]{2,1,0:T(1,128)S(1)} %bitcast.12), channel_id=1, replica_groups={{448,456,464,472,480,488,496,504,0,8,16,24,32,40,48,56,64,72,80,88,96,1..., dimensions={0} | all-to-all | bytes 327680 | tf_op jit(solution)/shard_map/all_to_all | solution.py:387
  46.2 0.9 %final.1 = (f32[1,256]{1,0:T(1,128)}, f32[1,256]{1,0:T(1,128)}, f32[1,256]{1,0:T(1,128)}, f32[8,128]{1,0:T(8,128)S(1)}) custom-call(f32[320,128]{1,0:T(8,128)S(1)} %bitcast.9, f32[8,256]{1,0:T(8,128)S(1)} %get-tuple-element.27.power_ref, f32[1,128]{1,0:T(1,128)S(1)} %get-tuple-element.28.start_ref, f32[1,256]{1,0:T(1,128)S(1)} %get-tuple-element.29.values_ref), custom_call_target="tpu_custom_call" | custom-call | tf_op jit(solution)/shard_map/final/pallas_call | solution.py:506
  47.1 8.9 %all_to_all.17 = f32[8,1,128]{2,1,0:T(1,128)S(1)} all-to-all(f32[8,1,128]{2,1,0:T(1,128)S(1)} %bitcast.13), channel_id=1, replica_groups={{0,1,2,3,4,5,6,7},{8,9,10,11,12,13,14,15},{16,17,18,19,20,21,22,23},{24..., dimensions={0} | all-to-all | bytes 8192 | tf_op jit(solution)/shard_map/all_to_all | solution.py:387
  56.0 0.6 %slice_reduce_fusion = f32[]{:T(128)} fusion(f32[8,1,128]{2,1,0:T(1,128)S(1)} %all_to_all.17), kind=kLoop, calls=%fused_computation | loop fusion | flops 7 | bytes 36 | tf_op jit(solution)/shard_map/reduce_sum | solution.py:519
Async XLA Ops:
  0.6 18.6 %copy-start = (f32[8,256]{1,0:T(8,128)S(1)}, f32[8,256]{1,0:T(8,128)}, u32[]{:S(2)}) copy-start(f32[8,256]{1,0:T(8,128)} %refs_1_.1) | copy-start | bytes 24580

commit v5 on v3

--- a/solution.py
+++ b/solution.py
@@ -18,7 +18,7 @@
 
 CHUNK = 64
 
-CONTRACT_LANES = (((1,), (1,)), ((), ()))
+TENSOR_FIRST, SEQ_FIRST, LAST_FIRST = 5, 40, 5
 
 
 def column(ref, shape):
@@ -209,6 +209,7 @@
 
 def local_kernel(
     hidden_width,
+    first,
     recv_ref,
     rewards_ref,
     gate_ref,
@@ -236,6 +237,7 @@
         ],
         axis=1,
     )
+    weight = in_order(weight, first)
     values = products * lax.rsqrt(squares / hidden_width + EPS_NORM)
     lane = lax.broadcasted_iota(jnp.int32, shape, 1)
     inner_next = jnp.where(lane < length - 1, pltpu.roll(values, length - 1, 1), 0.0)
@@ -280,11 +282,18 @@
         out_ref[TOKEN_ROWS * peer : TOKEN_ROWS * (peer + 1), :] = message[0:TOKEN_ROWS, :]
 
 
+def in_order(rows, first):
+    row = lax.broadcasted_iota(jnp.int32, rows.shape, 0)
+    swapped = jnp.where(row == 0, rows[first : first + 1], rows)
+    return jnp.where(row == first, rows[0:1], swapped)
+
+
 def full_sum(x):
     return jnp.sum(jnp.sum(x, axis=0, keepdims=True), axis=1, keepdims=True)
 
 
 def final_kernel(
+    first,
     recv_ref,
     power_ref,
     start_ref,
@@ -308,7 +317,7 @@
     blocks = recv_ref.shape[0] // TOKEN_ROWS
     rollouts = out_ref.shape[0]
     shape = (blocks, 128)
-    table = recv_ref[pl.ds(0, blocks, stride=TOKEN_ROWS), :]
+    table = in_order(recv_ref[pl.ds(0, blocks, stride=TOKEN_ROWS), :], first)
     row = lax.broadcasted_iota(jnp.int32, shape, 0)
     lane = lax.broadcasted_iota(jnp.int32, shape, 1)
 
@@ -347,8 +356,8 @@
         lanes = slice(128 * half, 128 * (half + 1))
         position = (lane + 128 * half).astype(jnp.float32)
         coef = jnp.where(position > own_done, power[:, lanes], 0.0)
-        local = recv_ref[pl.ds(1 + half, blocks, stride=TOKEN_ROWS), :]
-        ratio = recv_ref[pl.ds(3 + half, blocks, stride=TOKEN_ROWS), :]
+        local = in_order(recv_ref[pl.ds(1 + half, blocks, stride=TOKEN_ROWS), :], first)
+        ratio = in_order(recv_ref[pl.ds(3 + half, blocks, stride=TOKEN_ROWS), :], first)
         white = (local + coef * own_entering - mean) * scale
         clipped = jnp.clip(ratio, 1.0 - CLIP, 1.0 + CLIP)
         token = jnp.where(ratio > 0.0, -jnp.minimum(ratio * white, clipped * white), 0.0)
@@ -374,8 +383,10 @@
     return pltpu.VMEM(shape, jnp.float32)
 
 
-def exchange(x, axis):
-    return lax.all_to_all(x, axis, 0, 0, tiled=True)
+def exchange(x, axis, first):
+    order = list(range(lax.axis_size(axis)))
+    order[0], order[first] = order[first], order[0]
+    return lax.all_to_all(x, axis, 0, 0, axis_index_groups=[order], tiled=True)
 
 
 def run_head(
@@ -466,9 +477,9 @@
         trace_decay,
         bootstrap,
     )
-    got = exchange(sent.reshape(peers, 1, HEAD_ROWS * 128), "tensor")
+    got = exchange(sent.reshape(peers, 1, HEAD_ROWS * 128), "tensor", TENSOR_FIRST)
     values, sent = pl.pallas_call(
-        lambda *refs: local_kernel(width * peers, *refs),
+        partial(local_kernel, width * peers, TENSOR_FIRST),
         out_shape=(
             on_chip_shape((1, length)),
             on_chip_shape((blocks * TOKEN_ROWS, 128)),
@@ -491,10 +502,10 @@
             ),
         )
     )
-    got = exchange(sent.reshape(blocks, 1, TOKEN_ROWS * 128), "seq")
+    got = exchange(sent.reshape(blocks, 1, TOKEN_ROWS * 128), "seq", SEQ_FIRST)
     own_row = jax.ShapeDtypeStruct((1, length), jnp.float32)
     values, white, loss, sent = pl.pallas_call(
-        final_kernel,
+        partial(final_kernel, SEQ_FIRST),
         out_shape=(own_row, own_row, own_row, on_chip_shape((peers, 128))),
         in_specs=[VMEM] * 4,
         out_specs=(ANY, ANY, ANY, VMEM),
@@ -505,7 +516,7 @@
         ],
         name="final",
     )(*map(on_chip, (got.reshape(blocks * TOKEN_ROWS, 128), power, start, values)))
-    got = exchange(sent.reshape(peers, 1, 128), "tensor")
+    got = exchange(sent.reshape(peers, 1, 128), "tensor", LAST_FIRST)
     return values, white, loss, jnp.sum(got[:, 0, 0])
 
 

time: 61.4 us -> 53.6 us (0.87)
  blocking collectives: 54.3 us -> 46.5 us
    all_to_all x3, blocking collectives: 54.3 us -> 46.5 us  [exchange(): return lax.all_to_all(x, axis, 0, 0, axis_index_groups=[order], tiled=True)]
where the time goes in v5:
time: 53.6 us; the launch traced here: 53.4 us
  blocking collectives  46.5 us (87%)
  Pallas kernels  5.6 us (10%)
  between operations  0.67 us (1%)
  other arithmetic  0.61 us (1%)
    all_to_all x3, blocking collectives, exchange(): return lax.all_to_all(x, axis, 0, 0, axis_index_groups=[order], tiled=True)  46.5 us
    pallas_call x1, Pallas kernels, run_head(): pl.pallas_call(head_kernel, out_shape=(on_chip_shape((peers * HEAD_ROWS,...  3.83 us

profile of v5, /device:TPU:1, one launch (start us, length us, event | category | flops | bytes accessed | tf_op | source)
XLA Modules:
  0.0 53.4 jit_solution(8790383629377936155)
XLA Ops:
  0.6 0.0 copy-start
  0.6 3.8 %head.1 = (f32[320,128]{1,0:T(8,128)S(1)}, f32[8,256]{1,0:T(8,128)S(1)}, f32[64,256]{1,0:T(8,128)S(1)}, f32[8,256]{1,0:T(8,128)S(1)}, f32[8,256]{1,0:T(8,128)S(1...) custom-call(bf16[8,128]{1,0:T(8,128)(2,1)} %bitcast.14, ...), custom_call_target="tpu_custom_call" | custom-call | tf_op jit(solution)/shard_map/head/pallas_call | solution.py:408
  4.5 14.0 %all_to_all.15 = f32[8,1,5120]{2,1,0:T(1,128)S(1)} all-to-all(f32[8,1,5120]{2,1,0:T(1,128)S(1)} %bitcast.11), channel_id=1, replica_groups={{5,1,2,3,4,0,6,7},{13,9,10,11,12,8,14,15},{21,17,18,19,20,16,22,23},{29..., dimensions={0} | all-to-all | bytes 327680 | tf_op jit(solution)/shard_map/all_to_all | solution.py:389
  18.5 0.0 copy-done
  18.5 0.8 %local.1 = (f32[1,256]{1,0:T(1,128)S(1)}, f32[320,128]{1,0:T(8,128)S(1)}) custom-call(f32[320,128]{1,0:T(8,128)S(1)} %bitcast.10, f32[8,256]{1,0:T(8,128)S(1)} %copy-done, f32[8,256]{1,0:T(8,128)S(1)} %get-tuple-element.20.gate_ref, f32[64,256]{1,0:T(8,128)S(1)} %get-tuple-element.21.chain_ref, f32[8,256]{1,0:T(8,128)S(1)} %get-tuple-element.22.coef_ref, ...), custom_call_target="tpu_custom_call" | custom-call | tf_op jit(solution)/shard_map/local/pallas_call | solution.py:481
  19.4 25.1 %all_to_all.16 = f32[64,1,640]{2,1,0:T(1,128)S(1)} all-to-all(f32[64,1,640]{2,1,0:T(1,128)S(1)} %bitcast.12), channel_id=1, replica_groups={{320,8,16,24,32,40,48,56,64,72,80,88,96,104,112,120,128,136,144,152,160..., dimensions={0} | all-to-all | bytes 327680 | tf_op jit(solution)/shard_map/all_to_all | solution.py:389
  44.5 0.9 %final.1 = (f32[1,256]{1,0:T(1,128)}, f32[1,256]{1,0:T(1,128)}, f32[1,256]{1,0:T(1,128)}, f32[8,128]{1,0:T(8,128)S(1)}) custom-call(f32[320,128]{1,0:T(8,128)S(1)} %bitcast.9, f32[8,256]{1,0:T(8,128)S(1)} %get-tuple-element.27.power_ref, f32[1,128]{1,0:T(1,128)S(1)} %get-tuple-element.28.start_ref, f32[1,256]{1,0:T(1,128)S(1)} %get-tuple-element.29.values_ref), custom_call_target="tpu_custom_call" | custom-call | tf_op jit(solution)/shard_map/final/pallas_call | solution.py:507
  45.4 7.3 %all_to_all.17 = f32[8,1,128]{2,1,0:T(1,128)S(1)} all-to-all(f32[8,1,128]{2,1,0:T(1,128)S(1)} %bitcast.13), channel_id=1, replica_groups={{5,1,2,3,4,0,6,7},{13,9,10,11,12,8,14,15},{21,17,18,19,20,16,22,23},{29..., dimensions={0} | all-to-all | bytes 8192 | tf_op jit(solution)/shard_map/all_to_all | solution.py:389
  52.8 0.6 %slice_reduce_fusion = f32[]{:T(128)} fusion(f32[8,1,128]{2,1,0:T(1,128)S(1)} %all_to_all.17), kind=kLoop, calls=%fused_computation | loop fusion | flops 7 | bytes 36 | tf_op jit(solution)/shard_map/reduce_sum | solution.py:520
Async XLA Ops:
  0.6 17.9 %copy-start = (f32[8,256]{1,0:T(8,128)S(1)}, f32[8,256]{1,0:T(8,128)}, u32[]{:S(2)}) copy-start(f32[8,256]{1,0:T(8,128)} %rewards_ref.1) | copy-start | bytes 24580

commit v6 on v3

--- a/solution.py
+++ b/solution.py
@@ -18,7 +18,8 @@
 
 CHUNK = 64
 
-CONTRACT_LANES = (((1,), (1,)), ((), ()))
+TENSOR_ORDER = [5, 1, 2, 3, 4, 0, 6, 7]
+SEQ_RUNS = [5, 7, 3, 1, 0, 2, 4, 6]
 
 
 def column(ref, shape):
@@ -63,7 +64,9 @@
     discount_smem,
     trace_smem,
     bootstrap_smem,
-    fold_ref,
+    split_ref,
+    pick_ref,
+    sums_ref,
     arrived,
 ):
     rollouts, length, width = held.shape
@@ -89,18 +92,15 @@
     ]
     for copy in copies[:1] + small + copies[1:]:
         copy.start()
+    picked = lax.broadcasted_iota(jnp.int32, (3 * 128, 128), 0) % 128 // 64 * 8
+    picked = lax.broadcasted_iota(jnp.int32, (3 * 128, 128), 1) - picked
+    for r in range(rollouts):
+        pick_ref[r] = jnp.where(picked == r, 1.0, 0.0).astype(jnp.bfloat16)
     for copy in small:
         copy.wait()
 
     scaled = gain_ref[...].astype(jnp.float32) * weight_ref[...].astype(jnp.float32)
     small_lane = lax.broadcasted_iota(jnp.int32, (8, 128), 1)
-    levels = rollouts.bit_length() - 1
-    group = 64 >> levels
-
-    def fold(even, odd, distance):
-        even = even + pltpu.roll(even, 128 - distance, 1)
-        odd = odd + pltpu.roll(odd, distance, 1)
-        return jnp.where((small_lane[0:1] // distance) % 2 == 0, even, odd)
 
     def partial_sums(r, here):
         squares = products = jnp.zeros((CHUNK, 128), jnp.float32)
@@ -108,36 +108,25 @@
             wide = held[r, here, 128 * j : 128 * (j + 1)].astype(jnp.float32)
             squares = squares + wide * wide
             products = products + wide * scaled[j : j + 1, :]
-        folded, distance = fold(squares, products, 64), 32
-        for level in range(levels):
-            if not (r >> level) & 1:
-                fold_ref[level, here] = folded
-                return None
-            folded, distance = fold(fold_ref[level, here], folded, distance), distance // 2
-        return folded
-
-    def finish(half, folded):
-        turned = jnp.transpose(folded)
-        sublane = lax.broadcasted_iota(jnp.int32, (8, 128), 0)
-        for kind in range(2):
-            rows = []
-            for r in range(rollouts):
-                at = kind
-                for level in range(levels):
-                    at = 2 * at + (r >> level) % 2
-                rows.append(turned[group * at : group * (at + 1)])
-            distance = group // 2
-            while distance:
-                even, odd = rows[:distance], rows[distance:]
-                rows = []
-                for e, o in zip(even, odd, strict=True):
-                    e = e + pltpu.roll(e, 8 - distance, 0)
-                    o = o + pltpu.roll(o, distance, 0)
-                    rows.append(jnp.where((sublane // distance) % 2 == 0, e, o))
-                distance //= 2
+        left = small_lane[0:1] < 64
+        rest = jnp.where(left, squares, products)
+        rest = rest + pltpu.roll(jnp.where(left, products, squares), 64, 1)
+        for part in range(3):
+            coarse = rest.astype(jnp.bfloat16)
+            split_ref[r % 2, here, 128 * part : 128 * (part + 1)] = coarse
+            rest = rest - coarse.astype(jnp.float32)
+
+    def lane_sums(r):
+        sums = jnp.dot(split_ref[r % 2], pick_ref[r], preferred_element_type=jnp.float32)
+        sums_ref[...] = sums_ref[...] + sums if r else sums
+
+    def finish():
+        for half in range(length // 128):
+            turned = jnp.transpose(sums_ref[128 * half : 128 * (half + 1), :])
             for peer in range(peers):
-                at = HEAD_ROWS * peer + 8 * (2 * kind + half)
-                out_ref[at : at + 8, :] = rows[0]
+                for kind in range(2):
+                    at = HEAD_ROWS * peer + 8 * (2 * kind + half)
+                    out_ref[at : at + 8, :] = turned[8 * kind : 8 * (kind + 1)]
 
     shape = (rollouts, length)
     lane = lax.broadcasted_iota(jnp.int32, shape, 1)
@@ -198,13 +187,12 @@
         copies[r].wait()
         for piece in pieces[r]:
             piece()
-        for half in range(2):
-            folded = [
-                partial_sums(r, slice(first, first + CHUNK))
-                for first in range(128 * half, 128 * (half + 1), CHUNK)
-            ]
-            if r == rollouts - 1:
-                finish(half, jnp.concatenate(folded, axis=0))
+        if r:
+            lane_sums(r - 1)
+        for first in range(0, length, CHUNK):
+            partial_sums(r, slice(first, first + CHUNK))
+    lane_sums(rollouts - 1)
+    finish()
 
 
 def local_kernel(
@@ -236,6 +224,11 @@
         ],
         axis=1,
     )
+    slot = lax.broadcasted_iota(jnp.int32, shape, 0)
+    received = weight
+    for peer, member in enumerate(TENSOR_ORDER):
+        if peer != member:
+            weight = jnp.where(slot == member, received[peer : peer + 1], weight)
     values = products * lax.rsqrt(squares / hidden_width + EPS_NORM)
     lane = lax.broadcasted_iota(jnp.int32, shape, 1)
     inner_next = jnp.where(lane < length - 1, pltpu.roll(values, length - 1, 1), 0.0)
@@ -280,35 +273,30 @@
         out_ref[TOKEN_ROWS * peer : TOKEN_ROWS * (peer + 1), :] = message[0:TOKEN_ROWS, :]
 
 
+def seq_order(size):
+    runs = size // 8
+    order = SEQ_RUNS if runs == len(SEQ_RUNS) else range(runs)
+    return [8 * run + i for run in order for i in range(8)]
+
+
+def from_blocks(ref, at):
+    blocks = ref.shape[0] // TOKEN_ROWS
+    rows = ref[pl.ds(at, blocks, stride=TOKEN_ROWS), :]
+    order = seq_order(blocks)
+    slots = [order.index(8 * run) for run in range(blocks // 8)]
+    return jnp.concatenate([rows[slot : slot + 8] for slot in slots], axis=0)
+
+
 def full_sum(x):
     return jnp.sum(jnp.sum(x, axis=0, keepdims=True), axis=1, keepdims=True)
 
 
-def final_kernel(
-    recv_ref,
-    power_ref,
-    start_ref,
-    values_ref,
-    values_hbm,
-    white_hbm,
-    loss_hbm,
-    out_ref,
-    white_ref,
-    loss_ref,
-    sent,
-):
+def final_kernel(recv_ref, power_ref, start_ref, white_ref, loss_ref, out_ref):
     tensor, seq = lax.axis_index("tensor"), lax.axis_index("seq")
-    writes = [
-        pltpu.make_async_copy(source, target, sent.at[i])
-        for i, (source, target) in enumerate(
-            ((values_ref, values_hbm), (white_ref, white_hbm), (loss_ref, loss_hbm))
-        )
-    ]
-    writes[0].start()
     blocks = recv_ref.shape[0] // TOKEN_ROWS
     rollouts = out_ref.shape[0]
     shape = (blocks, 128)
-    table = recv_ref[pl.ds(0, blocks, stride=TOKEN_ROWS), :]
+    table = from_blocks(recv_ref, 0)
     row = lax.broadcasted_iota(jnp.int32, shape, 0)
     lane = lax.broadcasted_iota(jnp.int32, shape, 1)
 
@@ -347,17 +335,29 @@
         lanes = slice(128 * half, 128 * (half + 1))
         position = (lane + 128 * half).astype(jnp.float32)
         coef = jnp.where(position > own_done, power[:, lanes], 0.0)
-        local = recv_ref[pl.ds(1 + half, blocks, stride=TOKEN_ROWS), :]
-        ratio = recv_ref[pl.ds(3 + half, blocks, stride=TOKEN_ROWS), :]
+        local = from_blocks(recv_ref, 1 + half)
+        ratio = from_blocks(recv_ref, 3 + half)
         white = (local + coef * own_entering - mean) * scale
         clipped = jnp.clip(ratio, 1.0 - CLIP, 1.0 + CLIP)
         token = jnp.where(ratio > 0.0, -jnp.minimum(ratio * white, clipped * white), 0.0)
         loss = loss + token
         white_ref[:, lanes] = jnp.sum(jnp.where(mine_row, white, 0.0), axis=0, keepdims=True)
         loss_ref[:, lanes] = jnp.sum(jnp.where(mine_row, token, 0.0), axis=0, keepdims=True)
-    writes[1].start()
-    writes[2].start()
     out_ref[...] = jnp.broadcast_to(full_sum(loss) / count, out_ref.shape)
+
+
+def last_kernel(
+    values_ref, white_ref, loss_ref, recv_ref, values_hbm, white_hbm, loss_hbm, policy_ref, sent
+):
+    writes = [
+        pltpu.make_async_copy(source, target, sent.at[i])
+        for i, (source, target) in enumerate(
+            ((values_ref, values_hbm), (white_ref, white_hbm), (loss_ref, loss_hbm))
+        )
+    ]
+    for write in writes:
+        write.start()
+    policy_ref[0, 0] = jnp.sum(recv_ref[:, 0:1])
     for write in writes:
         write.wait()
 
@@ -374,8 +374,8 @@
     return pltpu.VMEM(shape, jnp.float32)
 
 
-def exchange(x, axis):
-    return lax.all_to_all(x, axis, 0, 0, tiled=True)
+def exchange(x, axis, order):
+    return lax.all_to_all(x, axis, 0, 0, axis_index_groups=[order], tiled=True)
 
 
 def run_head(
@@ -420,7 +420,9 @@
             pltpu.SMEM(discount.shape, f32),
             pltpu.SMEM(trace_decay.shape, f32),
             pltpu.SMEM(bootstrap.shape, f32),
-            pltpu.VMEM((3, length, 128), f32),
+            pltpu.VMEM((2, length, 3 * 128), jnp.bfloat16),
+            pltpu.VMEM((rollouts, 3 * 128, 128), jnp.bfloat16),
+            pltpu.VMEM((length, 128), f32),
             pltpu.SemaphoreType.DMA((rollouts + 9,)),
         ],
         name="head",
@@ -466,9 +468,9 @@
         trace_decay,
         bootstrap,
     )
-    got = exchange(sent.reshape(peers, 1, HEAD_ROWS * 128), "tensor")
+    got = exchange(sent.reshape(peers, 1, HEAD_ROWS * 128), "tensor", TENSOR_ORDER)
     values, sent = pl.pallas_call(
-        lambda *refs: local_kernel(width * peers, *refs),
+        partial(local_kernel, width * peers),
         out_shape=(
             on_chip_shape((1, length)),
             on_chip_shape((blocks * TOKEN_ROWS, 128)),
@@ -491,22 +493,29 @@
             ),
         )
     )
-    got = exchange(sent.reshape(blocks, 1, TOKEN_ROWS * 128), "seq")
+    got = exchange(sent.reshape(blocks, 1, TOKEN_ROWS * 128), "seq", seq_order(blocks))
+    white, loss, sent = pl.pallas_call(
+        final_kernel,
+        out_shape=(
+            on_chip_shape((1, length)),
+            on_chip_shape((1, length)),
+            on_chip_shape((peers, 128)),
+        ),
+        in_specs=[VMEM] * 3,
+        out_specs=(VMEM, VMEM, VMEM),
+        name="final",
+    )(*map(on_chip, (got.reshape(blocks * TOKEN_ROWS, 128), power, start)))
+    got = exchange(sent.reshape(peers, 1, 128), "tensor", TENSOR_ORDER)
     own_row = jax.ShapeDtypeStruct((1, length), jnp.float32)
-    values, white, loss, sent = pl.pallas_call(
-        final_kernel,
-        out_shape=(own_row, own_row, own_row, on_chip_shape((peers, 128))),
+    values, white, loss, policy = pl.pallas_call(
+        last_kernel,
+        out_shape=(own_row, own_row, own_row, jax.ShapeDtypeStruct((1, 1), jnp.float32)),
         in_specs=[VMEM] * 4,
-        out_specs=(ANY, ANY, ANY, VMEM),
-        scratch_shapes=[
-            pltpu.VMEM((1, length), jnp.float32),
-            pltpu.VMEM((1, length), jnp.float32),
-            pltpu.SemaphoreType.DMA((3,)),
-        ],
-        name="final",
-    )(*map(on_chip, (got.reshape(blocks * TOKEN_ROWS, 128), power, start, values)))
-    got = exchange(sent.reshape(peers, 1, 128), "tensor")
-    return values, white, loss, jnp.sum(got[:, 0, 0])
+        out_specs=(ANY, ANY, ANY, pl.BlockSpec(memory_space=pltpu.SMEM)),
+        scratch_shapes=[pltpu.SemaphoreType.DMA((3,))],
+        name="last",
+    )(*map(on_chip, (values, white, loss, got.reshape(peers, 128))))
+    return values, white, loss, policy.reshape(())
 
 
 def solution(mesh):

time: 61.4 us -> 53.1 us (0.86)
  blocking collectives: 54.3 us -> 46.3 us
    all_to_all x3, blocking collectives: 54.3 us -> 46.3 us  [exchange(): return lax.all_to_all(x, axis, 0, 0, axis_index_groups=[order], tiled=True)]
    pallas_call x2 -> x3, Pallas kernels: 1.77 us -> 2.37 us  [the longest x1 1.11 us: shards(): pl.pallas_call(last_kernel, out_shape=(own_row, own_row, own_row, jax.Sha...]
where the time goes in v6:
time: 53.1 us; the launch traced here: 52.9 us
  blocking collectives  46.3 us (87%)
  Pallas kernels  5.89 us (11%)
  between operations  0.66 us (1%)
    all_to_all x3, blocking collectives, exchange(): return lax.all_to_all(x, axis, 0, 0, axis_index_groups=[order], tiled=True)  46.3 us
    pallas_call x1, Pallas kernels, run_head(): pl.pallas_call(head_kernel, out_shape=(on_chip_shape((peers * HEAD_ROWS,...  3.52 us
    pallas_call x1, Pallas kernels, shards(): pl.pallas_call(last_kernel, out_shape=(own_row, own_row, own_row, jax.Sha...  1.11 us

profile of v6, /device:TPU:1, one launch (start us, length us, event | category | flops | bytes accessed | tf_op | source)
XLA Modules:
  0.0 52.9 jit_solution(14119528441342232786)
XLA Ops:
  0.6 0.0 copy-start
  0.6 3.5 %head.1 = (f32[320,128]{1,0:T(8,128)S(1)}, f32[8,256]{1,0:T(8,128)S(1)}, f32[64,256]{1,0:T(8,128)S(1)}, f32[8,256]{1,0:T(8,128)S(1)}, f32[8,256]{1,0:T(8,128)S(1...) custom-call(bf16[8,128]{1,0:T(8,128)(2,1)} %bitcast.17, ...), custom_call_target="tpu_custom_call" | custom-call | tf_op jit(solution)/shard_map/head/pallas_call | solution.py:397
  4.2 14.0 %all_to_all.15 = f32[8,1,5120]{2,1,0:T(1,128)S(1)} all-to-all(f32[8,1,5120]{2,1,0:T(1,128)S(1)} %bitcast.13), channel_id=1, replica_groups={{5,1,2,3,4,0,6,7},{13,9,10,11,12,8,14,15},{21,17,18,19,20,16,22,23},{29..., dimensions={0} | all-to-all | bytes 327680 | tf_op jit(solution)/shard_map/all_to_all | solution.py:378
  18.2 0.0 copy-done
  18.2 0.8 %local.1 = (f32[1,256]{1,0:T(1,128)S(1)}, f32[320,128]{1,0:T(8,128)S(1)}) custom-call(f32[320,128]{1,0:T(8,128)S(1)} %bitcast.11, f32[8,256]{1,0:T(8,128)S(1)} %copy-done, f32[8,256]{1,0:T(8,128)S(1)} %get-tuple-element.23.gate_ref, f32[64,256]{1,0:T(8,128)S(1)} %get-tuple-element.24.chain_ref, f32[8,256]{1,0:T(8,128)S(1)} %get-tuple-element.25.coef_ref, ...), custom_call_target="tpu_custom_call" | custom-call | tf_op jit(solution)/shard_map/local/pallas_call | solution.py:472
  19.1 24.8 %all_to_all.16 = f32[64,1,640]{2,1,0:T(1,128)S(1)} all-to-all(f32[64,1,640]{2,1,0:T(1,128)S(1)} %bitcast.14), channel_id=1, replica_groups={{320,328,336,344,352,360,368,376,448,456,464,472,480,488,496,504,192,20..., dimensions={0} | all-to-all | bytes 327680 | tf_op jit(solution)/shard_map/all_to_all | solution.py:378
  43.9 0.4 final.1
  44.3 7.5 %all_to_all.17 = f32[8,1,128]{2,1,0:T(1,128)S(1)} all-to-all(f32[8,1,128]{2,1,0:T(1,128)S(1)} %bitcast.16), channel_id=1, replica_groups={{5,1,2,3,4,0,6,7},{13,9,10,11,12,8,14,15},{21,17,18,19,20,16,22,23},{29..., dimensions={0} | all-to-all | bytes 8192 | tf_op jit(solution)/shard_map/all_to_all | solution.py:378
  51.8 1.1 %last.1 = (f32[1,256]{1,0:T(1,128)}, f32[1,256]{1,0:T(1,128)}, f32[1,256]{1,0:T(1,128)}, f32[1,1]{1,0:T(1,128)}) custom-call(f32[1,256]{1,0:T(1,128)S(1)} %get-tuple-element.29.values_ref, f32[1,256]{1,0:T(1,128)S(1)} %get-tuple-element.33.white_ref, f32[1,256]{1,0:T(1,128)S(1)} %get-tuple-element.34.loss_ref, f32[8,128]{1,0:T(8,128)S(1)} %bitcast.15), custom_call_target="tpu_custom_call" | custom-call | tf_op jit(solution)/shard_map/last/pallas_call | solution.py:510
Async XLA Ops:
  0.6 17.6 %copy-start = (f32[8,256]{1,0:T(8,128)S(1)}, f32[8,256]{1,0:T(8,128)}, u32[]{:S(2)}) copy-start(f32[8,256]{1,0:T(8,128)} %rewards_ref.1) | copy-start | bytes 24580

commit v7 on v6

--- a/solution.py
+++ b/solution.py
@@ -12,14 +12,14 @@
 CLIP = 0.2
 
 HEAD_ROWS = 40
-TOKEN_ROWS = 5
+TOKEN_ROWS = 3
 WIDTH = 16
 OFFSET, SLOPE, COUNT, MEAN_L, MEAN_C, VAR_L, COV, VAR_C, LAST_DONE = range(9)
 
 CHUNK = 64
 
-TENSOR_ORDER = [5, 1, 2, 3, 4, 0, 6, 7]
-SEQ_RUNS = [5, 7, 3, 1, 0, 2, 4, 6]
+ALONG_Z = 16
+TENSOR_FIRST, SEQ_FIRST, PAIR_FIRST = 5, 41, 13
 
 
 def column(ref, shape):
@@ -206,6 +206,7 @@
     trace_ref,
     ratio_ref,
     values_ref,
+    own_ref,
     out_ref,
 ):
     me = lax.axis_index("tensor")
@@ -224,11 +225,7 @@
         ],
         axis=1,
     )
-    slot = lax.broadcasted_iota(jnp.int32, shape, 0)
-    received = weight
-    for peer, member in enumerate(TENSOR_ORDER):
-        if peer != member:
-            weight = jnp.where(slot == member, received[peer : peer + 1], weight)
+    weight = in_order(weight, TENSOR_FIRST)
     values = products * lax.rsqrt(squares / hidden_width + EPS_NORM)
     lane = lax.broadcasted_iota(jnp.int32, shape, 1)
     inner_next = jnp.where(lane < length - 1, pltpu.roll(values, length - 1, 1), 0.0)
@@ -264,37 +261,45 @@
     own_local = jnp.sum(jnp.where(mine, local, 0.0), axis=0, keepdims=True)
     values_ref[...] = jnp.sum(jnp.where(mine, values, 0.0), axis=0, keepdims=True)
     row = lax.broadcasted_iota(jnp.int32, (8, 128), 0)
-    message = jnp.where(row == 0, summary, 0.0)
-    message = jnp.where(row == 1, own_local[:, :128], message)
-    message = jnp.where(row == 2, own_local[:, 128:], message)
-    message = jnp.where(row == 3, ratio_ref[:, :128], message)
-    message = jnp.where(row == 4, ratio_ref[:, 128:], message)
-    for peer in range(out_ref.shape[0] // TOKEN_ROWS):
-        out_ref[TOKEN_ROWS * peer : TOKEN_ROWS * (peer + 1), :] = message[0:TOKEN_ROWS, :]
-
-
-def seq_order(size):
-    runs = size // 8
-    order = SEQ_RUNS if runs == len(SEQ_RUNS) else range(runs)
-    return [8 * run + i for run in order for i in range(8)]
+    own_ref[...] = own_local
+    messages = []
+    for half in range(2):
+        lanes = slice(128 * half, 128 * (half + 1))
+        message = jnp.where(row == 1, own_local[:, lanes], ratio_ref[:, lanes])
+        messages.append(jnp.where(row == 0, summary, message)[0:TOKEN_ROWS])
+    blocks = out_ref.shape[0] // TOKEN_ROWS
+    for slot, member in enumerate(order_from(blocks, SEQ_FIRST)):
+        half = member // ALONG_Z % 2
+        out_ref[TOKEN_ROWS * slot : TOKEN_ROWS * (slot + 1), :] = messages[half]
+
+
+def order_from(size, first):
+    order = list(range(size))
+    order[0], order[first] = order[first], order[0]
+    return order
+
+
+def in_order(rows, first):
+    row = lax.broadcasted_iota(jnp.int32, rows.shape, 0)
+    swapped = jnp.where(row == 0, rows[first : first + 1], rows)
+    return jnp.where(row == first, rows[0:1], swapped)
 
 
 def from_blocks(ref, at):
     blocks = ref.shape[0] // TOKEN_ROWS
-    rows = ref[pl.ds(at, blocks, stride=TOKEN_ROWS), :]
-    order = seq_order(blocks)
-    slots = [order.index(8 * run) for run in range(blocks // 8)]
-    return jnp.concatenate([rows[slot : slot + 8] for slot in slots], axis=0)
+    return in_order(ref[pl.ds(at, blocks, stride=TOKEN_ROWS), :], SEQ_FIRST)
 
 
 def full_sum(x):
     return jnp.sum(jnp.sum(x, axis=0, keepdims=True), axis=1, keepdims=True)
 
 
-def final_kernel(recv_ref, power_ref, start_ref, white_ref, loss_ref, out_ref):
+def final_kernel(
+    recv_ref, power_ref, start_ref, own_ref, ratio_ref, white_ref, loss_ref, out_ref
+):
     tensor, seq = lax.axis_index("tensor"), lax.axis_index("seq")
     blocks = recv_ref.shape[0] // TOKEN_ROWS
-    rollouts = out_ref.shape[0]
+    rollouts = power_ref.shape[0]
     shape = (blocks, 128)
     table = from_blocks(recv_ref, 0)
     row = lax.broadcasted_iota(jnp.int32, shape, 0)
@@ -329,35 +334,53 @@
     own_entering = lane_sum(jnp.where(mine, entering, 0.0))
     own_done = lane_sum(jnp.where(mine, stat(LAST_DONE), 0.0))
     power = power_ref[pl.ds(tensor, 1), :]
-    loss = jnp.zeros(shape, jnp.float32)
-    mine_row = row == seq
-    for half in range(2):
-        lanes = slice(128 * half, 128 * (half + 1))
-        position = (lane + 128 * half).astype(jnp.float32)
-        coef = jnp.where(position > own_done, power[:, lanes], 0.0)
-        local = from_blocks(recv_ref, 1 + half)
-        ratio = from_blocks(recv_ref, 3 + half)
-        white = (local + coef * own_entering - mean) * scale
+
+    def losses(local, ratio, coef, from_later):
+        white = (local + coef * from_later - mean) * scale
         clipped = jnp.clip(ratio, 1.0 - CLIP, 1.0 + CLIP)
-        token = jnp.where(ratio > 0.0, -jnp.minimum(ratio * white, clipped * white), 0.0)
-        loss = loss + token
-        white_ref[:, lanes] = jnp.sum(jnp.where(mine_row, white, 0.0), axis=0, keepdims=True)
-        loss_ref[:, lanes] = jnp.sum(jnp.where(mine_row, token, 0.0), axis=0, keepdims=True)
-    out_ref[...] = jnp.broadcast_to(full_sum(loss) / count, out_ref.shape)
+        return white, jnp.where(ratio > 0.0, -jnp.minimum(ratio * white, clipped * white), 0.0)
+
+    half = seq // ALONG_Z % 2
+    power_half = jnp.where(half == 0, power[:, :128], power[:, 128:])
+    coef = jnp.where((lane + 128 * half).astype(jnp.float32) > own_done, power_half, 0.0)
+    _, token = losses(from_blocks(recv_ref, 1), from_blocks(recv_ref, 2), coef, own_entering)
+    out_ref[...] = jnp.broadcast_to(full_sum(token) / count, out_ref.shape)
+
+    here = row[:, 0:1] == seq
+    position = lax.broadcasted_iota(jnp.int32, power.shape, 1).astype(jnp.float32)
+    own_done = jnp.sum(jnp.where(here, own_done, 0.0), axis=0, keepdims=True)
+    own_entering = jnp.sum(jnp.where(here, own_entering, 0.0), axis=0, keepdims=True)
+    coef = jnp.where(position > own_done, power, 0.0)
+    white_ref[...], loss_ref[...] = losses(own_ref[...], ratio_ref[...], coef, own_entering)
 
 
 def last_kernel(
-    values_ref, white_ref, loss_ref, recv_ref, values_hbm, white_hbm, loss_hbm, policy_ref, sent
+    values_ref,
+    white_ref,
+    loss_ref,
+    recv_ref,
+    values_hbm,
+    white_hbm,
+    loss_hbm,
+    policy_hbm,
+    policy_ref,
+    sent,
 ):
     writes = [
         pltpu.make_async_copy(source, target, sent.at[i])
         for i, (source, target) in enumerate(
-            ((values_ref, values_hbm), (white_ref, white_hbm), (loss_ref, loss_hbm))
+            (
+                (values_ref, values_hbm),
+                (white_ref, white_hbm),
+                (loss_ref, loss_hbm),
+                (policy_ref, policy_hbm),
+            )
         )
     ]
-    for write in writes:
+    for write in writes[:3]:
         write.start()
     policy_ref[0, 0] = jnp.sum(recv_ref[:, 0:1])
+    writes[3].start()
     for write in writes:
         write.wait()
 
@@ -374,8 +397,17 @@
     return pltpu.VMEM(shape, jnp.float32)
 
 
-def exchange(x, axis, order):
-    return lax.all_to_all(x, axis, 0, 0, axis_index_groups=[order], tiled=True)
+def exchange(x, axis, groups):
+    return lax.all_to_all(x, axis, 0, 0, axis_index_groups=groups, tiled=True)
+
+
+def pair_groups(blocks, peers):
+    groups = []
+    for first in range(0, blocks, 2 * ALONG_Z):
+        for block in range(first, first + ALONG_Z):
+            members = [b * peers + i for b in (block, block + ALONG_Z) for i in range(peers)]
+            groups.append([members[i] for i in order_from(2 * peers, PAIR_FIRST)])
+    return groups
 
 
 def run_head(
@@ -468,15 +500,16 @@
         trace_decay,
         bootstrap,
     )
-    got = exchange(sent.reshape(peers, 1, HEAD_ROWS * 128), "tensor", TENSOR_ORDER)
-    values, sent = pl.pallas_call(
+    got = exchange(sent.reshape(peers, 1, HEAD_ROWS * 128), "tensor", [order_from(peers, TENSOR_FIRST)])
+    values, own, sent = pl.pallas_call(
         partial(local_kernel, width * peers),
         out_shape=(
+            on_chip_shape((1, length)),
             on_chip_shape((1, length)),
             on_chip_shape((blocks * TOKEN_ROWS, 128)),
         ),
         in_specs=[VMEM] * 8,
-        out_specs=(VMEM, VMEM),
+        out_specs=(VMEM,) * 3,
         name="local",
     )(
         *map(
@@ -493,28 +526,29 @@
             ),
         )
     )
-    got = exchange(sent.reshape(blocks, 1, TOKEN_ROWS * 128), "seq", seq_order(blocks))
+    got = exchange(sent.reshape(blocks, 1, TOKEN_ROWS * 128), "seq", [order_from(blocks, SEQ_FIRST)])
     white, loss, sent = pl.pallas_call(
         final_kernel,
         out_shape=(
             on_chip_shape((1, length)),
             on_chip_shape((1, length)),
-            on_chip_shape((peers, 128)),
+            on_chip_shape((2 * peers, 128)),
         ),
-        in_specs=[VMEM] * 3,
+        in_specs=[VMEM] * 5,
         out_specs=(VMEM, VMEM, VMEM),
         name="final",
-    )(*map(on_chip, (got.reshape(blocks * TOKEN_ROWS, 128), power, start)))
-    got = exchange(sent.reshape(peers, 1, 128), "tensor", TENSOR_ORDER)
+    )(*map(on_chip, (got.reshape(blocks * TOKEN_ROWS, 128), power, start, own, ratio)))
+    groups = pair_groups(blocks, peers)
+    got = exchange(sent.reshape(2 * peers, 1, 128), ("seq", "tensor"), groups)
     own_row = jax.ShapeDtypeStruct((1, length), jnp.float32)
     values, white, loss, policy = pl.pallas_call(
         last_kernel,
         out_shape=(own_row, own_row, own_row, jax.ShapeDtypeStruct((1, 1), jnp.float32)),
         in_specs=[VMEM] * 4,
-        out_specs=(ANY, ANY, ANY, pl.BlockSpec(memory_space=pltpu.SMEM)),
-        scratch_shapes=[pltpu.SemaphoreType.DMA((3,))],
+        out_specs=(ANY,) * 4,
+        scratch_shapes=[pltpu.SMEM((1, 1), jnp.float32), pltpu.SemaphoreType.DMA((4,))],
         name="last",
-    )(*map(on_chip, (values, white, loss, got.reshape(peers, 128))))
+    )(*map(on_chip, (values, white, loss, got.reshape(2 * peers, 128))))
     return values, white, loss, policy.reshape(())
 
 

time: 53.1 us -> 50.8 us (0.957)
  blocking collectives: 46.3 us -> 44.5 us
    all_to_all x3, blocking collectives: 46.3 us -> 44.5 us  [exchange(): return lax.all_to_all(x, axis, 0, 0, axis_index_groups=groups, tiled=True)]
where the time goes in v7:
time: 50.8 us; the launch traced here: 50.6 us
  blocking collectives  44.5 us (88%)
  Pallas kernels  5.42 us (11%)
  between operations  0.66 us (1%)
    all_to_all x3, blocking collectives, exchange(): return lax.all_to_all(x, axis, 0, 0, axis_index_groups=groups, tiled=True)  44.5 us
    pallas_call x1, Pallas kernels, run_head(): pl.pallas_call(head_kernel, out_shape=(on_chip_shape((peers * HEAD_ROWS,...  3.52 us

profile of v7, /device:TPU:1, one launch (start us, length us, event | category | flops | bytes accessed | tf_op | source)
XLA Modules:
  0.0 50.6 jit_solution(3236202978364051305)
XLA Ops:
  0.6 0.0 copy-start
  0.6 3.5 %head.1 = (f32[320,128]{1,0:T(8,128)S(1)}, f32[8,256]{1,0:T(8,128)S(1)}, f32[64,256]{1,0:T(8,128)S(1)}, f32[8,256]{1,0:T(8,128)S(1)}, f32[8,256]{1,0:T(8,128)S(1...) custom-call(bf16[8,128]{1,0:T(8,128)(2,1)} %bitcast.17, ...), custom_call_target="tpu_custom_call" | custom-call | tf_op jit(solution)/shard_map/head/pallas_call | solution.py:429
  4.2 14.0 %all_to_all.15 = f32[8,1,5120]{2,1,0:T(1,128)S(1)} all-to-all(f32[8,1,5120]{2,1,0:T(1,128)S(1)} %bitcast.13), channel_id=1, replica_groups={{5,1,2,3,4,0,6,7},{13,9,10,11,12,8,14,15},{21,17,18,19,20,16,22,23},{29..., dimensions={0} | all-to-all | bytes 327680 | tf_op jit(solution)/shard_map/all_to_all | solution.py:401
  18.2 0.0 copy-done
  18.2 0.8 %local.1 = (f32[1,256]{1,0:T(1,128)S(1)}, f32[1,256]{1,0:T(1,128)S(1)}, f32[192,128]{1,0:T(8,128)S(1)}) custom-call(f32[320,128]{1,0:T(8,128)S(1)} %bitcast.11, f32[8,256]{1,0:T(8,128)S(1)} %copy-done, f32[8,256]{1,0:T(8,128)S(1)} %get-tuple-element.24.gate_ref, f32[64,256]{1,0:T(8,128)S(1)} %get-tuple-element.25.chain_ref, ...), custom_call_target="tpu_custom_call" | custom-call | tf_op jit(solution)/shard_map/local/pallas_call | solution.py:504
  19.1 21.8 %all_to_all.16 = f32[64,1,384]{2,1,0:T(1,128)S(1)} all-to-all(f32[64,1,384]{2,1,0:T(1,128)S(1)} %bitcast.14), channel_id=1, replica_groups={{328,8,16,24,32,40,48,56,64,72,80,88,96,104,112,120,128,136,144,152,160..., dimensions={0} | all-to-all | bytes 196608 | tf_op jit(solution)/shard_map/all_to_all | solution.py:401
  40.9 0.4 final.1
  41.3 8.6 %all_to_all.17 = f32[16,1,128]{2,1,0:T(1,128)S(1)} all-to-all(f32[16,1,128]{2,1,0:T(1,128)S(1)} %bitcast.16), channel_id=1, replica_groups={{133,1,2,3,4,5,6,7,128,129,130,131,132,0,134,135},{141,9,10,11,12,13,14..., dimensions={0} | all-to-all | bytes 16384 | tf_op jit(solution)/shard_map/all_to_all | solution.py:401
  49.9 0.7 %last.1 = (f32[1,256]{1,0:T(1,128)}, f32[1,256]{1,0:T(1,128)}, f32[1,256]{1,0:T(1,128)}, f32[1,1]{1,0:T(1,128)}) custom-call(f32[1,256]{1,0:T(1,128)S(1)} %get-tuple-element.30.values_ref, f32[1,256]{1,0:T(1,128)S(1)} %get-tuple-element.35.white_ref, f32[1,256]{1,0:T(1,128)S(1)} %get-tuple-element.36.loss_ref, f32[16,128]{1,0:T(8,128)S(1)} %bitcast.15), custom_call_target="tpu_custom_call" | custom-call | tf_op jit(solution)/shard_map/last/pallas_call | solution.py:544
Async XLA Ops:
  0.6 17.6 %copy-start = (f32[8,256]{1,0:T(8,128)S(1)}, f32[8,256]{1,0:T(8,128)}, u32[]{:S(2)}) copy-start(f32[8,256]{1,0:T(8,128)} %rewards_ref.1) | copy-start | bytes 24580

commit v8 on v7

--- a/solution.py
+++ b/solution.py
@@ -11,7 +11,7 @@
 EPS_WHITE = 1e-08
 CLIP = 0.2
 
-HEAD_ROWS = 40
+HEAD_ROWS = 34
 TOKEN_ROWS = 3
 WIDTH = 16
 OFFSET, SLOPE, COUNT, MEAN_L, MEAN_C, VAR_L, COV, VAR_C, LAST_DONE = range(9)
@@ -48,6 +48,7 @@
     out_ref,
     gate_ref,
     chain_ref,
+    triple_ref,
     coef_ref,
     power_ref,
     fixed_ref,
@@ -134,10 +135,10 @@
     def piece_own():
         mask = mask_ref[...].astype(jnp.float32)
         ratio_ref[...] = mask * jnp.exp(new_ref[...] - old_ref[...])
-        row = lax.broadcasted_iota(jnp.int32, (8, 128), 0)
-        rest = jnp.where(row == 0, mask[:, :128], jnp.where(row == 1, mask[:, 128:], 0.0))
         for peer in range(peers):
-            out_ref[HEAD_ROWS * peer + 32 : HEAD_ROWS * (peer + 1), :] = rest
+            at = HEAD_ROWS * peer + 32
+            out_ref[at : at + 1, :] = mask[:, :128]
+            out_ref[at + 1 : at + 2, :] = mask[:, 128:]
         start_lane = lax.broadcasted_iota(jnp.int32, (1, 128), 1)
         start = jnp.full((1, 128), bootstrap_smem[0], jnp.float32)
         for r in range(1, rollouts):
@@ -165,6 +166,13 @@
         coef_ref[...] = chain / column(trace_smem, shape)
         fixed_ref[...] = jnp.where(small_lane == SLOPE, chain[:, 0:1], fixed_ref[...])
 
+    def piece_triple(at):
+        step = 1 << at
+        chain = chain_ref[rollouts * at : rollouts * (at + 1), :]
+        later = pltpu.roll(chain, length - 2 * step, 1)
+        triple = chain_ref[rollouts * (at + 1) : rollouts * (at + 2), :] * later
+        triple_ref[rollouts * (at // 2) : rollouts * (at // 2 + 1), :] = triple
+
     def piece_power():
         discount = column(discount_smem, shape)
         left = length - 1 - lane
@@ -180,6 +188,8 @@
     pieces[0] = [piece_chain_start]
     for at in range(steps):
         pieces[1 + at * (rollouts - 2) // steps].append(partial(piece_chain, at))
+    for at in range(0, steps, 2):
+        pieces[rollouts - 1].append(partial(piece_triple, at))
     pieces[0].append(piece_own)
     pieces[rollouts - 2].append(piece_power)
 
@@ -201,6 +211,7 @@
     rewards_ref,
     gate_ref,
     chain_ref,
+    triple_ref,
     coef_ref,
     fixed_ref,
     trace_ref,
@@ -232,9 +243,17 @@
     local = rewards_ref[...] + gate_ref[...] * inner_next - values
     step, at = 1, 0
     while step < length:
-        later = jnp.where(lane < length - step, pltpu.roll(local, length - step, 1), 0.0)
-        local = local + chain_ref[rollouts * at : rollouts * (at + 1), :] * later
-        step, at = 2 * step, at + 1
+        factors = (
+            chain_ref[rollouts * at : rollouts * (at + 1), :],
+            chain_ref[rollouts * (at + 1) : rollouts * (at + 2), :],
+            triple_ref[rollouts * (at // 2) : rollouts * (at // 2 + 1), :],
+        )
+        later = [
+            factor * jnp.where(lane < length - k * step, pltpu.roll(local, length - k * step, 1), 0.0)
+            for k, factor in enumerate(factors, 1)
+        ]
+        local = (local + later[0]) + (later[1] + later[2])
+        step, at = 4 * step, at + 2
     coef = coef_ref[...]
     count = lane_sum(weight)
     safe = 1.0 / jnp.maximum(count, 1.0)
@@ -432,6 +451,7 @@
             on_chip_shape((peers * HEAD_ROWS, 128)),
             on_chip_shape((rollouts, length)),
             on_chip_shape((rollouts * steps, length)),
+            on_chip_shape((rollouts * steps // 2, length)),
             on_chip_shape((rollouts, length)),
             on_chip_shape((rollouts, length)),
             on_chip_shape((rollouts, 128)),
@@ -440,7 +460,7 @@
             on_chip_shape((1, 128)),
         ),
         in_specs=[ANY] * 10,
-        out_specs=(VMEM,) * 9,
+        out_specs=(VMEM,) * 10,
         scratch_shapes=[
             pltpu.VMEM(hidden.shape, hidden.dtype),
             pltpu.VMEM((width // 128, 128), norm_gain.dtype),
@@ -487,7 +507,7 @@
 ):
     rollouts, length, width = hidden.shape
     peers, blocks = lax.axis_size("tensor"), lax.axis_size("seq")
-    sent, gate, chain, coef, power, fixed, trace, ratio, start = run_head(
+    sent, gate, chain, triple, coef, power, fixed, trace, ratio, start = run_head(
         peers,
         hidden,
         norm_gain,
@@ -508,7 +528,7 @@
             on_chip_shape((1, length)),
             on_chip_shape((blocks * TOKEN_ROWS, 128)),
         ),
-        in_specs=[VMEM] * 8,
+        in_specs=[VMEM] * 9,
         out_specs=(VMEM,) * 3,
         name="local",
     )(
@@ -519,6 +539,7 @@
                 rewards,
                 gate,
                 chain,
+                triple,
                 coef,
                 fixed,
                 trace,

time: 50.8 us -> 50.3 us (level)
  no operation moved by 1% of the time
where the time goes in v8:
time: 50.3 us; the launch traced here: 50.1 us
  blocking collectives  44.2 us (88%)
  Pallas kernels  5.23 us (10%)
  between operations  0.66 us (1%)
    all_to_all x3, blocking collectives, exchange(): return lax.all_to_all(x, axis, 0, 0, axis_index_groups=groups, tiled=True)  44.2 us
    pallas_call x1, Pallas kernels, run_head(): pl.pallas_call(head_kernel, out_shape=(on_chip_shape((peers * HEAD_ROWS,...  3.52 us

profile of v8, /device:TPU:1, one launch (start us, length us, event | category | flops | bytes accessed | tf_op | source)
XLA Modules:
  0.0 50.1 jit_solution(2852320572326049956)
XLA Ops:
  0.6 0.0 copy-start
  0.6 3.5 %head.1 = (f32[272,128]{1,0:T(8,128)S(1)}, f32[8,256]{1,0:T(8,128)S(1)}, f32[64,256]{1,0:T(8,128)S(1)}, f32[32,256]{1,0:T(8,128)S(1)}, f32[8,256]{1,0:T(8,128)S(...) custom-call(bf16[8,128]{1,0:T(8,128)(2,1)} %bitcast.17, ...), custom_call_target="tpu_custom_call" | custom-call | tf_op jit(solution)/shard_map/head/pallas_call | solution.py:448
  4.2 13.8 %all_to_all.15 = f32[8,1,4352]{2,1,0:T(1,128)S(1)} all-to-all(f32[8,1,4352]{2,1,0:T(1,128)S(1)} %bitcast.13), channel_id=1, replica_groups={{5,1,2,3,4,0,6,7},{13,9,10,11,12,8,14,15},{21,17,18,19,20,16,22,23},{29..., dimensions={0} | all-to-all | bytes 278528 | tf_op jit(solution)/shard_map/all_to_all | solution.py:420
  18.0 0.0 copy-done
  18.0 0.6 %local.1 = (f32[1,256]{1,0:T(1,128)S(1)}, f32[1,256]{1,0:T(1,128)S(1)}, f32[192,128]{1,0:T(8,128)S(1)}) custom-call(f32[272,128]{1,0:T(8,128)S(1)} %bitcast.11, f32[8,256]{1,0:T(8,128)S(1)} %copy-done, f32[8,256]{1,0:T(8,128)S(1)} %get-tuple-element.25.gate_ref, f32[64,256]{1,0:T(8,128)S(1)} %get-tuple-element.26.chain_ref, ...), custom_call_target="tpu_custom_call" | custom-call | tf_op jit(solution)/shard_map/local/pallas_call | solution.py:524
  18.6 21.8 %all_to_all.16 = f32[64,1,384]{2,1,0:T(1,128)S(1)} all-to-all(f32[64,1,384]{2,1,0:T(1,128)S(1)} %bitcast.14), channel_id=1, replica_groups={{328,8,16,24,32,40,48,56,64,72,80,88,96,104,112,120,128,136,144,152,160..., dimensions={0} | all-to-all | bytes 196608 | tf_op jit(solution)/shard_map/all_to_all | solution.py:420
  40.5 0.4 final.1
  40.9 8.6 %all_to_all.17 = f32[16,1,128]{2,1,0:T(1,128)S(1)} all-to-all(f32[16,1,128]{2,1,0:T(1,128)S(1)} %bitcast.16), channel_id=1, replica_groups={{133,1,2,3,4,5,6,7,128,129,130,131,132,0,134,135},{141,9,10,11,12,13,14..., dimensions={0} | all-to-all | bytes 16384 | tf_op jit(solution)/shard_map/all_to_all | solution.py:420
  49.4 0.7 %last.1 = (f32[1,256]{1,0:T(1,128)}, f32[1,256]{1,0:T(1,128)}, f32[1,256]{1,0:T(1,128)}, f32[1,1]{1,0:T(1,128)}) custom-call(f32[1,256]{1,0:T(1,128)S(1)} %get-tuple-element.32.values_ref, f32[1,256]{1,0:T(1,128)S(1)} %get-tuple-element.37.white_ref, f32[1,256]{1,0:T(1,128)S(1)} %get-tuple-element.38.loss_ref, f32[16,128]{1,0:T(8,128)S(1)} %bitcast.15), custom_call_target="tpu_custom_call" | custom-call | tf_op jit(solution)/shard_map/last/pallas_call | solution.py:565
Async XLA Ops:
  0.6 17.3 %copy-start = (f32[8,256]{1,0:T(8,128)S(1)}, f32[8,256]{1,0:T(8,128)}, u32[]{:S(2)}) copy-start(f32[8,256]{1,0:T(8,128)} %rewards_ref.1) | copy-start | bytes 24580

commit v9 on v8

--- a/solution.py
+++ b/solution.py
@@ -19,7 +19,8 @@
 CHUNK = 64
 
 ALONG_Z = 16
-TENSOR_FIRST, SEQ_FIRST, PAIR_FIRST = 5, 41, 13
+SEQ_FIRST, PAIR_FIRST = 41, 13
+TENSOR_ORDER = [5, 4, 7, 6, 3, 2, 1, 0]
 
 
 def column(ref, shape):
@@ -236,7 +237,10 @@
         ],
         axis=1,
     )
-    weight = in_order(weight, TENSOR_FIRST)
+    member_row = lax.broadcasted_iota(jnp.int32, shape, 0)
+    received, weight = weight, jnp.zeros(shape, jnp.float32)
+    for slot, member in enumerate(TENSOR_ORDER):
+        weight = jnp.where(member_row == member, received[slot : slot + 1], weight)
     values = products * lax.rsqrt(squares / hidden_width + EPS_NORM)
     lane = lax.broadcasted_iota(jnp.int32, shape, 1)
     inner_next = jnp.where(lane < length - 1, pltpu.roll(values, length - 1, 1), 0.0)
@@ -520,7 +524,7 @@
         trace_decay,
         bootstrap,
     )
-    got = exchange(sent.reshape(peers, 1, HEAD_ROWS * 128), "tensor", [order_from(peers, TENSOR_FIRST)])
+    got = exchange(sent.reshape(peers, 1, HEAD_ROWS * 128), "tensor", [TENSOR_ORDER])
     values, own, sent = pl.pallas_call(
         partial(local_kernel, width * peers),
         out_shape=(

time: 50.3 us -> 50 us (level)
  no operation moved by 1% of the time
where the time goes in v9:
time: 50 us; the launch traced here: 49.8 us
  blocking collectives  44 us (88%)
  Pallas kernels  5.23 us (10%)
  between operations  0.66 us (1%)
    all_to_all x3, blocking collectives, exchange(): return lax.all_to_all(x, axis, 0, 0, axis_index_groups=groups, tiled=True)  44 us
    pallas_call x1, Pallas kernels, run_head(): pl.pallas_call(head_kernel, out_shape=(on_chip_shape((peers * HEAD_ROWS,...  3.52 us

profile of v9, /device:TPU:1, one launch (start us, length us, event | category | flops | bytes accessed | tf_op | source)
XLA Modules:
  0.0 49.8 jit_solution(1658545979703341589)
XLA Ops:
  0.6 0.0 copy-start
  0.6 3.5 %head.1 = (f32[272,128]{1,0:T(8,128)S(1)}, f32[8,256]{1,0:T(8,128)S(1)}, f32[64,256]{1,0:T(8,128)S(1)}, f32[32,256]{1,0:T(8,128)S(1)}, f32[8,256]{1,0:T(8,128)S(...) custom-call(bf16[8,128]{1,0:T(8,128)(2,1)} %bitcast.17, ...), custom_call_target="tpu_custom_call" | custom-call | tf_op jit(solution)/shard_map/head/pallas_call | solution.py:452
  4.2 13.4 %all_to_all.15 = f32[8,1,4352]{2,1,0:T(1,128)S(1)} all-to-all(f32[8,1,4352]{2,1,0:T(1,128)S(1)} %bitcast.13), channel_id=1, replica_groups={{5,4,7,6,3,2,1,0},{13,12,15,14,11,10,9,8},{21,20,23,22,19,18,17,16},{29..., dimensions={0} | all-to-all | bytes 278528 | tf_op jit(solution)/shard_map/all_to_all | solution.py:424
  17.6 0.0 copy-done
  17.6 0.6 %local.1 = (f32[1,256]{1,0:T(1,128)S(1)}, f32[1,256]{1,0:T(1,128)S(1)}, f32[192,128]{1,0:T(8,128)S(1)}) custom-call(f32[272,128]{1,0:T(8,128)S(1)} %bitcast.11, f32[8,256]{1,0:T(8,128)S(1)} %copy-done, f32[8,256]{1,0:T(8,128)S(1)} %get-tuple-element.25.gate_ref, f32[64,256]{1,0:T(8,128)S(1)} %get-tuple-element.26.chain_ref, ...), custom_call_target="tpu_custom_call" | custom-call | tf_op jit(solution)/shard_map/local/pallas_call | solution.py:528
  18.2 21.6 %all_to_all.16 = f32[64,1,384]{2,1,0:T(1,128)S(1)} all-to-all(f32[64,1,384]{2,1,0:T(1,128)S(1)} %bitcast.14), channel_id=1, replica_groups={{328,8,16,24,32,40,48,56,64,72,80,88,96,104,112,120,128,136,144,152,160..., dimensions={0} | all-to-all | bytes 196608 | tf_op jit(solution)/shard_map/all_to_all | solution.py:424
  39.8 0.4 final.1
  40.2 9.0 %all_to_all.17 = f32[16,1,128]{2,1,0:T(1,128)S(1)} all-to-all(f32[16,1,128]{2,1,0:T(1,128)S(1)} %bitcast.16), channel_id=1, replica_groups={{133,1,2,3,4,5,6,7,128,129,130,131,132,0,134,135},{141,9,10,11,12,13,14..., dimensions={0} | all-to-all | bytes 16384 | tf_op jit(solution)/shard_map/all_to_all | solution.py:424
  49.2 0.7 %last.1 = (f32[1,256]{1,0:T(1,128)}, f32[1,256]{1,0:T(1,128)}, f32[1,256]{1,0:T(1,128)}, f32[1,1]{1,0:T(1,128)}) custom-call(f32[1,256]{1,0:T(1,128)S(1)} %get-tuple-element.32.values_ref, f32[1,256]{1,0:T(1,128)S(1)} %get-tuple-element.37.white_ref, f32[1,256]{1,0:T(1,128)S(1)} %get-tuple-element.38.loss_ref, f32[16,128]{1,0:T(8,128)S(1)} %bitcast.15), custom_call_target="tpu_custom_call" | custom-call | tf_op jit(solution)/shard_map/last/pallas_call | solution.py:569
Async XLA Ops:
  0.6 16.9 %copy-start = (f32[8,256]{1,0:T(8,128)S(1)}, f32[8,256]{1,0:T(8,128)}, u32[]{:S(2)}) copy-start(f32[8,256]{1,0:T(8,128)} %rewards_ref.1) | copy-start | bytes 24580

commit v10 on v9

--- a/solution.py
+++ b/solution.py
@@ -19,7 +19,8 @@
 CHUNK = 64
 
 ALONG_Z = 16
-SEQ_FIRST, PAIR_FIRST = 41, 13
+SEQ_FIRST = 41
+PAIR_ORDER = [13, 12, 15, 14, 11, 10, 9, 8, 5, 4, 7, 6, 3, 2, 1, 0]
 TENSOR_ORDER = [5, 4, 7, 6, 3, 2, 1, 0]
 
 
@@ -429,7 +430,7 @@
     for first in range(0, blocks, 2 * ALONG_Z):
         for block in range(first, first + ALONG_Z):
             members = [b * peers + i for b in (block, block + ALONG_Z) for i in range(peers)]
-            groups.append([members[i] for i in order_from(2 * peers, PAIR_FIRST)])
+            groups.append([members[i] for i in PAIR_ORDER])
     return groups
 
 

time: 50 us -> 50.1 us (level)
  no operation moved by 1% of the time
where the time goes in v10:
time: 50.1 us; the launch traced here: 49.9 us
  blocking collectives  44 us (88%)
  Pallas kernels  5.23 us (10%)
  between operations  0.66 us (1%)
    all_to_all x3, blocking collectives, exchange(): return lax.all_to_all(x, axis, 0, 0, axis_index_groups=groups, tiled=True)  44 us
    pallas_call x1, Pallas kernels, run_head(): pl.pallas_call(head_kernel, out_shape=(on_chip_shape((peers * HEAD_ROWS,...  3.52 us

profile of v10, /device:TPU:1, one launch (start us, length us, event | category | flops | bytes accessed | tf_op | source)
XLA Modules:
  0.0 49.9 jit_solution(6102418610496366894)
XLA Ops:
  0.6 0.0 copy-start
  0.6 3.5 %head.1 = (f32[272,128]{1,0:T(8,128)S(1)}, f32[8,256]{1,0:T(8,128)S(1)}, f32[64,256]{1,0:T(8,128)S(1)}, f32[32,256]{1,0:T(8,128)S(1)}, f32[8,256]{1,0:T(8,128)S(...) custom-call(bf16[8,128]{1,0:T(8,128)(2,1)} %bitcast.17, ...), custom_call_target="tpu_custom_call" | custom-call | tf_op jit(solution)/shard_map/head/pallas_call | solution.py:453
  4.2 13.4 %all_to_all.15 = f32[8,1,4352]{2,1,0:T(1,128)S(1)} all-to-all(f32[8,1,4352]{2,1,0:T(1,128)S(1)} %bitcast.13), channel_id=1, replica_groups={{5,4,7,6,3,2,1,0},{13,12,15,14,11,10,9,8},{21,20,23,22,19,18,17,16},{29..., dimensions={0} | all-to-all | bytes 278528 | tf_op jit(solution)/shard_map/all_to_all | solution.py:425
  17.6 0.0 copy-done
  17.6 0.6 %local.1 = (f32[1,256]{1,0:T(1,128)S(1)}, f32[1,256]{1,0:T(1,128)S(1)}, f32[192,128]{1,0:T(8,128)S(1)}) custom-call(f32[272,128]{1,0:T(8,128)S(1)} %bitcast.11, f32[8,256]{1,0:T(8,128)S(1)} %copy-done, f32[8,256]{1,0:T(8,128)S(1)} %get-tuple-element.25.gate_ref, f32[64,256]{1,0:T(8,128)S(1)} %get-tuple-element.26.chain_ref, ...), custom_call_target="tpu_custom_call" | custom-call | tf_op jit(solution)/shard_map/local/pallas_call | solution.py:529
  18.2 21.6 %all_to_all.16 = f32[64,1,384]{2,1,0:T(1,128)S(1)} all-to-all(f32[64,1,384]{2,1,0:T(1,128)S(1)} %bitcast.14), channel_id=1, replica_groups={{328,8,16,24,32,40,48,56,64,72,80,88,96,104,112,120,128,136,144,152,160..., dimensions={0} | all-to-all | bytes 196608 | tf_op jit(solution)/shard_map/all_to_all | solution.py:425
  39.8 0.4 final.1
  40.2 9.0 %all_to_all.17 = f32[16,1,128]{2,1,0:T(1,128)S(1)} all-to-all(f32[16,1,128]{2,1,0:T(1,128)S(1)} %bitcast.16), channel_id=1, replica_groups={{133,132,135,134,131,130,129,128,5,4,7,6,3,2,1,0},{141,140,143,142,139,..., dimensions={0} | all-to-all | bytes 16384 | tf_op jit(solution)/shard_map/all_to_all | solution.py:425
  49.2 0.7 %last.1 = (f32[1,256]{1,0:T(1,128)}, f32[1,256]{1,0:T(1,128)}, f32[1,256]{1,0:T(1,128)}, f32[1,1]{1,0:T(1,128)}) custom-call(f32[1,256]{1,0:T(1,128)S(1)} %get-tuple-element.32.values_ref, f32[1,256]{1,0:T(1,128)S(1)} %get-tuple-element.37.white_ref, f32[1,256]{1,0:T(1,128)S(1)} %get-tuple-element.38.loss_ref, f32[16,128]{1,0:T(8,128)S(1)} %bitcast.15), custom_call_target="tpu_custom_call" | custom-call | tf_op jit(solution)/shard_map/last/pallas_call | solution.py:570
Async XLA Ops:
  0.6 16.9 %copy-start = (f32[8,256]{1,0:T(8,128)S(1)}, f32[8,256]{1,0:T(8,128)}, u32[]{:S(2)}) copy-start(f32[8,256]{1,0:T(8,128)} %rewards_ref.1) | copy-start | bytes 24580
